TPU v7x, 128 devices: a whole 4x4x4 slice. The times are simulated.
128 devices in a mesh: gx: 4 (over y), gy: 8 (over x_lo, z), gz: 4 (over x_hi, core).
Axes of the slice: x: 4 (x_hi: 2, x_lo: 2; x = x_hi * 2 + x_lo), y: 4, z: 4, core: 2. Of those that a mesh axis runs over, the one named last changes fastest.
Arguments:
- populations: float32 [19, 32, 128, 512], P(None, 'gx', 'gy', 'gz'), may hold values from 0 to 1, as said below
- solid_fraction: float32 [32, 128, 512], P('gx', 'gy', 'gz'), may hold values from 0 to 1
- intersection: int32 [32, 128, 512], P('gx', 'gy', 'gz'), may hold values from 0 to 256, as said below
- touch: int32 [4, 8, 4, 256], P('gx', 'gy', 'gz'), may hold values from 0 to 3455, as said below
- particles: float32 [4, 8, 4, 6, 128], P('gx', 'gy', 'gz'), may hold values from -8 to 8, as said below
- contacts: int32 [4, 8, 4, 12, 128], P('gx', 'gy', 'gz'), may hold values from 0 to 3456, as said below
- dest_code: int32 [4, 8, 4, 128], P('gx', 'gy', 'gz'), may hold values from 4 to 22, as said below
- dest_slot: int32 [4, 8, 4, 128], P('gx', 'gy', 'gz'), may hold values from 0 to 127, as said below
Outputs:
- populations_next: float32 [19, 32, 128, 512], P(None, 'gx', 'gy', 'gz')
- particles_next: float32 [4, 8, 4, 6, 128], P('gx', 'gy', 'gz')
Inputs may be any that keep to these rules, and one draw needn't show every extreme that they name: intersection = 256 marks a cell that no sphere covers; otherwise a touch slot of the cell's block. `touch`: entry o * 128 + s names slot s of the block at offset o of the 27 neighbouring blocks, offsets ordered with x slowest; the entries of one block are distinct and name every slot of the block itself. `contacts`: 3456 marks an empty entry. `dest_code`: a sphere stays (code 13) or moves one block along one axis (codes 4, 10, 12, 14, 16, 22), never out of the mesh; every slot of every block receives exactly one record. `dest_slot`: see dest_code. `populations`: every population is positive. `particles`: positions, in radii from the block centre, lie within the block's half widths; speeds lie within -1.5 to 1.5.
All inputs are finite; a program needn't handle non-finite values.
Results may differ from a plain program's by a relative error of at most 0.000076.
Values sent between devices are 32-bit elements; how exact they have to be, the bound alone decides.
A program may use at most 128 MiB of HBM per device.

v0:
```python
import math

import jax
import jax.numpy as jnp
from jax import lax
from jax.sharding import PartitionSpec as P

R = 8


LATTICE = [
    (0, 0, 0),
    (1, 0, 0),
    (-1, 0, 0),
    (0, 1, 0),
    (0, -1, 0),
    (0, 0, 1),
    (0, 0, -1),
    (1, 1, 0),
    (-1, -1, 0),
    (1, -1, 0),
    (-1, 1, 0),
    (1, 0, 1),
    (-1, 0, -1),
    (1, 0, -1),
    (-1, 0, 1),
    (0, 1, 1),
    (0, -1, -1),
    (0, 1, -1),
    (0, -1, 1),
]
OPPOSITE = [0, 2, 1, 4, 3, 6, 5, 8, 7, 10, 9, 12, 11, 14, 13, 16, 15, 18, 17]
WEIGHTS = [1.0 / 3.0] + [1.0 / 18.0] * 6 + [1.0 / 36.0] * 12
RELAX_TIME = 0.8
SPEED_UNIT = 0.05
FORCE_SCALE = 0.1
CONTACT_GAIN = 1.0
GRAVITY_STEP = 0.1


def padded(shard, sides, width):
    for axis, dim in sides:
        peers, length = (lax.axis_size(axis), shard.shape[dim])
        up = [(i, (i + 1) % peers) for i in range(peers - 1)]
        down = [(j, i) for i, j in up]
        last = lax.slice_in_dim(shard, length - width, length, axis=dim)
        first = lax.slice_in_dim(shard, 0, width, axis=dim)
        before = lax.ppermute(last, axis, up)
        after = lax.ppermute(first, axis, down)
        shard = jnp.concatenate([before, shard, after], axis=dim)
    return shard


def equilibrium(density, velocity):
    square = velocity[0] * velocity[0] + velocity[1] * velocity[1] + velocity[2] * velocity[2]
    result = []
    for vector, weight in zip(LATTICE, WEIGHTS):
        projected = vector[0] * velocity[0] + vector[1] * velocity[1] + vector[2] * velocity[2]
        result.append(
            weight * density * (1.0 + 3.0 * projected + 4.5 * projected * projected - 1.5 * square)
        )
    return jnp.stack(result)


def collide(populations, solid_weight, solid_velocity):
    lattice_table = jnp.array(LATTICE, jnp.float32)
    density = jnp.sum(populations, axis=0)
    momentum = jnp.tensordot(lattice_table.T, populations, axes=1, precision=lax.Precision.HIGHEST)
    velocity = momentum / density
    fluid_eq = equilibrium(density, velocity)
    solid_eq = equilibrium(density, solid_velocity)
    mirrored = jnp.stack([populations[mirror_index] for mirror_index in OPPOSITE])
    fluid_mirror = jnp.stack([fluid_eq[mirror_index] for mirror_index in OPPOSITE])
    exchange_term = mirrored - populations + solid_eq - fluid_mirror
    relaxed = (
        populations
        - (1.0 - solid_weight) / RELAX_TIME * (populations - fluid_eq)
        + solid_weight * exchange_term
    )
    cell_force = -jnp.tensordot(
        lattice_table.T, solid_weight * exchange_term, axes=1, precision=lax.Precision.HIGHEST
    )
    return (relaxed, cell_force)


def block_offsets(entries, slots_each, span_x, span_y, span_z, radius):
    block_code = jnp.arange(entries, dtype=jnp.int32) // slots_each
    return jnp.stack(
        [
            (block_code // 9 - 1).astype(jnp.float32) * (span_x / radius),
            (block_code // 3 % 3 - 1).astype(jnp.float32) * (span_y / radius),
            (block_code % 3 - 1).astype(jnp.float32) * (span_z / radius),
        ]
    )


def moving_along(dimension):
    return [direction for direction, vector in enumerate(LATTICE) if vector[dimension] != 0]


def pick_moving(current, dimension):
    return jnp.stack([current[direction] for direction in moving_along(dimension)])


def shift_moving(current, widened, dimension):
    length = current.shape[dimension + 1]
    moving = moving_along(dimension)
    result = []
    for direction, vector in enumerate(LATTICE):
        if vector[dimension] != 0:
            position = moving.index(direction)
            result.append(
                lax.slice_in_dim(
                    widened[position],
                    1 - vector[dimension],
                    1 - vector[dimension] + length,
                    axis=dimension,
                )
            )
        else:
            result.append(current[direction])
    return jnp.stack(result)


def fold_ends(blocks_out, widened):
    return blocks_out[1] + widened[0] + widened[3]


def deliver(blocks_out):
    folded_x = fold_ends(
        blocks_out, padded(jnp.stack([blocks_out[0], blocks_out[2]]), (("gx", 0),), 1)
    )
    folded_y = fold_ends(folded_x, padded(jnp.stack([folded_x[0], folded_x[2]]), (("gy", 0),), 1))
    return fold_ends(folded_y, padded(jnp.stack([folded_y[0], folded_y[2]]), (("gz", 0),), 1))


def touch_sums(cell_force, intersection, touches):
    count = intersection.size
    width = math.gcd(count, 16384)
    turns = count // width
    block_forces = jnp.moveaxis(cell_force.reshape(3, turns, width), 1, 0)
    block_slots = intersection.reshape(turns, width)
    labels = jnp.arange(touches + 1, dtype=jnp.int32)

    def add_block(running, block_pair):
        block_force, block_slot = block_pair
        onehot = (block_slot[None, :] == labels[:, None]).astype(jnp.float32)
        return (
            running + jnp.einsum("dc,kc->dk", block_force, onehot, precision=lax.Precision.HIGHEST),
            None,
        )

    running, unused = lax.scan(
        add_block, jnp.zeros((3, touches + 1), jnp.float32), (block_forces, block_slots)
    )
    return running[:, :touches]


def body(
    populations, solid_fraction, intersection, touch, particles, contacts, dest_code, dest_slot
):
    span_x, span_y, span_z = (populations.shape[1], populations.shape[2], populations.shape[3])
    particle_slots = particles.shape[4]
    touches = touch.shape[3]
    neighbours = contacts.shape[3]
    entries = 27 * particle_slots
    nearby = padded(particles, (("gx", 0), ("gy", 1), ("gz", 2)), 1)
    records_near = jnp.transpose(nearby.reshape(27, 6, particle_slots), (1, 0, 2)).reshape(
        6, entries
    )
    touch_rows = touch.reshape(touches)
    touch_velocity = jnp.concatenate(
        [jnp.take(records_near[3:6], touch_rows, axis=1), jnp.zeros((3, 1), jnp.float32)], axis=1
    )
    solid_velocity = SPEED_UNIT * jnp.take(touch_velocity, intersection, axis=1)
    solid_weight = jnp.where(
        intersection < touches,
        solid_fraction * (RELAX_TIME - 0.5) / (1.0 - solid_fraction + (RELAX_TIME - 0.5)),
        jnp.float32(0.0),
    )
    relaxed, cell_force = collide(populations, solid_weight, solid_velocity)
    pulled = shift_moving(relaxed, padded(pick_moving(relaxed, 0), (("gx", 1),), 1), 0)
    pulled = shift_moving(pulled, padded(pick_moving(pulled, 1), (("gy", 2),), 1), 1)
    pulled = shift_moving(pulled, padded(pick_moving(pulled, 2), (("gz", 3),), 1), 2)
    total_x = lax.axis_size("gx") * span_x
    total_y = lax.axis_size("gy") * span_y
    total_z = lax.axis_size("gz") * span_z
    coord_x = lax.axis_index("gx") * span_x + jnp.arange(span_x, dtype=jnp.int32)[:, None, None]
    coord_y = lax.axis_index("gy") * span_y + jnp.arange(span_y, dtype=jnp.int32)[None, :, None]
    coord_z = lax.axis_index("gz") * span_z + jnp.arange(span_z, dtype=jnp.int32)[None, None, :]
    passed = []
    for direction, vector in enumerate(LATTICE):
        inside = (
            (coord_x - vector[0] >= 0)
            & (coord_x - vector[0] < total_x)
            & (coord_y - vector[1] >= 0)
            & (coord_y - vector[1] < total_y)
            & (coord_z - vector[2] >= 0)
            & (coord_z - vector[2] < total_z)
        )
        passed.append(jnp.where(inside, pulled[direction], relaxed[OPPOSITE[direction]]))
    populations_next = jnp.stack(passed)
    touch_force = touch_sums(cell_force, intersection, touches)
    entry_ids = jnp.arange(entries, dtype=jnp.int32)
    picking = (touch_rows[:, None] == entry_ids[None, :]).astype(jnp.float32)
    spread = jnp.dot(touch_force, picking, precision=lax.Precision.HIGHEST)
    force_blocks = jnp.transpose(spread.reshape(3, 27, particle_slots), (1, 0, 2)).reshape(
        3, 3, 3, 3, particle_slots
    )
    hydro = deliver(force_blocks)
    offsets = block_offsets(entries + 1, particle_slots, span_x, span_y, span_z, R)
    partner_table = (
        jnp.concatenate([records_near[0:3], jnp.zeros((3, 1), jnp.float32)], axis=1) + offsets
    )
    contact_rows = contacts.reshape(neighbours, particle_slots)
    partner = jnp.take(partner_table, contact_rows, axis=1)
    own_records = particles.reshape(6, particle_slots)
    separation = own_records[0:3, None, :] - partner
    valid = (contact_rows < entries).astype(jnp.float32)
    square = jnp.sum(separation * separation, axis=0)
    soften = 1.0 + 0.25 * square
    strength = CONTACT_GAIN * valid / (soften * soften)
    contact_force = jnp.sum(separation * strength[None], axis=1)
    gravity = jnp.array([0.0, 0.0, GRAVITY_STEP], jnp.float32)
    velocity_new = own_records[3:6] + FORCE_SCALE * hydro + contact_force - gravity[:, None]
    position_new = own_records[0:3] + velocity_new * (SPEED_UNIT / R)
    dest_codes = dest_code.reshape(particle_slots)
    code_ids = jnp.arange(27, dtype=jnp.int32)
    routing = (dest_codes[None, :] == code_ids[:, None]).astype(jnp.float32)
    placing = (
        dest_slot.reshape(particle_slots)[:, None]
        == jnp.arange(particle_slots, dtype=jnp.int32)[None, :]
    ).astype(jnp.float32)
    code_shift = block_offsets(27, 1, span_x, span_y, span_z, R)
    moved_position = position_new[None] - code_shift.T[:, :, None]
    candidates = jnp.concatenate(
        [moved_position, jnp.broadcast_to(velocity_new[None], (27, 3, particle_slots))], axis=1
    )
    candidates = candidates * routing[:, None, :]
    record_blocks = jnp.einsum("cwp,pt->cwt", candidates, placing, precision=lax.Precision.HIGHEST)
    arrived = deliver(record_blocks.reshape(3, 3, 3, 6, particle_slots))
    return (populations_next, arrived.reshape(1, 1, 1, 6, particle_slots))


def solution(mesh):
    placed = (
        P(None, "gx", "gy", "gz"),
        P("gx", "gy", "gz"),
        P("gx", "gy", "gz"),
        P("gx", "gy", "gz", None),
        P("gx", "gy", "gz", None, None),
        P("gx", "gy", "gz", None, None),
        P("gx", "gy", "gz", None),
        P("gx", "gy", "gz", None),
    )
    return jax.shard_map(
        body,
        mesh=mesh,
        in_specs=placed,
        out_specs=(P(None, "gx", "gy", "gz"), P("gx", "gy", "gz", None, None)),
        check_vma=False,
    )
```

profile of v0, /device:TPU:105, one launch (start us, length us, event | category | flops | bytes accessed | tf_op | source)
XLA Modules:
  0.0 240.1 jit_solution(16522510927179137941)
XLA Ops:
  0.7 3.3 %collective-permute-start = (f32[1,1,1,6,128]{4,2,3,1,0:T(1,128)}, f32[1,1,1,6,128]{4,2,3,1,0:T(1,128)S(1)}, u32[]{:S(2)}, u32[]{:S(2)}) collective-permute-start(f32[1,1,1,6,128]{4,2,3,1,0:T(1,128)} %param.14), channel_id=1, source_target_pairs={{0,32},{32,64},{64,96},{1,33},{33,65},{65,97},{2,34},{34,66},{66,9... | collective-permute-start | bytes 9224 | tf_op jit(solution)/shard_map/ppermute | solution.py:48
  4.0 2.1 collective-permute-start.1
  6.1 0.9 compare_select_fusion
  6.9 0.9 compare_and_fusion
  9.4 1.3 compare_and_fusion.1
  12.1 1.2 compare_and_fusion.5
  13.9 0.8 constant_dynamic-update-slice_fusion.37
  14.8 1.4 reduce_sum.29
  16.2 1.6 fusion.7
  21.4 1.9 collective-permute-start.2
  23.4 3.4 %collective-permute-start.3 = (f32[3,1,1,6,128]{4,2,3,1,0:T(1,128)S(1)}, f32[3,1,1,6,128]{4,2,3,1,0:T(1,128)S(1)}, u32[]{:S(2)}, u32[]{:S(2)}) collective-permute-start(f32[3,1,1,6,128]{4,2,3,1,0:T(1,128)S(1)} %constant_dynamic-update-slice_fusion.38), channel_id=1, source_target_pairs={{4,0},{8,4},{12,8},{16,12},{20,16},{24,20},{28,24},{5,1},{9,5},{13... | collective-permute-start | bytes 27656 | tf_op jit(solution)/shard_map/ppermute | solution.py:49
  27.3 2.5 %collective-permute-done.3 = f32[3,1,1,6,128]{4,2,3,1,0:T(1,128)S(1)} collective-permute-done((f32[3,1,1,6,128]{4,2,3,1,0:T(1,128)S(1)}, f32[3,1,1,6,128]{4,2,3,1,0:T(1,128)S(1)}, u32[]{:S(2)}, u32[]{:S(2)}) %collective-permute-start.3) | collective-permute-done | bytes 9248 | tf_op jit(solution)/shard_map/ppermute | solution.py:49
  29.9 6.9 %collective-permute-start.4 = (f32[3,3,1,6,128]{4,2,3,1,0:T(1,128)S(1)}, f32[3,3,1,6,128]{4,2,3,1,0:T(1,128)S(1)}, u32[]{:S(2)}, u32[]{:S(2)}) collective-permute-start(f32[3,3,1,6,128]{4,2,3,1,0:T(1,128)S(1)} %pad_maximum_fusion.10), channel_id=1, source_target_pairs={{0,1},{1,2},{2,3},{4,5},{5,6},{6,7},{8,9},{9,10},{10,11},{12,13},{... | collective-permute-start | bytes 82952 | tf_op jit(solution)/shard_map/ppermute | solution.py:48
  36.8 1.9 collective-permute-start.5
  39.3 1.8 copy.279
  41.9 1.6 collective-permute-done.5
  44.3 1.4 copy.263
  45.7 1.5 gather_fusion
  47.1 1.0 select_bitcast_fusion
  48.2 60.2 %gather_fusion.1 = f32[16384,3]{1,0:T(8,128)} fusion(f32[3,257]{0,1:T(8,128)S(1)} %concatenate.42, s32[16384]{0:T(1024)} %broadcast_clamp_fusion), kind=kCustom, calls=%fused_computation.1 | custom fusion | bytes 458752 | tf_op jit(solution)/shard_map/jit(_take)/gather | solution.py:175
  108.3 5.2 %copy.287 = f32[8,16,128,3]{2,1,0,3:T(8,128)S(1)} copy(f32[8,16,128,3]{3,2,1,0:T(8,128)} %bitcast.426) | data formatting | bytes 393216 | tf_op jit(solution)/shard_map/jit(_take)/gather | solution.py:175
  115.3 1.1 copy-done.2
  117.1 1.8 fusion.9
  118.9 7.4 %fusion = f32[3,256]{1,0:T(4,128)S(1)} fusion(f32[3,16384]{1,0:T(4,128)S(1)} %bitcast.437, s32[16384]{0:T(1024)S(1)} %bitcast.433), kind=kOutput, calls=%fused_computation.4 | convolution fusion | flops 159383552 | bytes 265216 | tf_op jit(solution)/shard_map/while/body/eval_jaxpr/dc,kc->dk/dot_general | solution.py:149
  126.4 1.3 fusion.12
  127.7 3.2 %collective-permute-start.12 = (f32[1,3,3,3,128]{4,0,3,2,1:T(1,128)S(1)}, f32[1,3,3,3,128]{4,0,3,2,1:T(1,128)S(1)}, u32[]{:S(2)}, u32[]{:S(2)}) collective-permute-start(f32[1,3,3,3,128]{4,0,3,2,1:T(1,128)S(1)} %copy.273), channel_id=1, source_target_pairs={{0,32},{32,64},{64,96},{1,33},{33,65},{65,97},{2,34},{34,66},{66,9... | collective-permute-start | bytes 41480 | tf_op jit(solution)/shard_map/ppermute | solution.py:48
  130.9 2.1 collective-permute-start.13
  133.0 1.8 copy.278
  135.5 3.4 %pad_add_fusion = f32[3,3457]{0,1:T(8,128)} fusion(f32[3,3457]{0,1:T(8,128)} %copy.279, f32[3,3456]{0,1:T(8,128)} %bitcast.427), kind=kLoop, calls=%fused_computation.9 | loop fusion | flops 10371 | bytes 124440 | tf_op jit(solution)/shard_map/add | solution.py:213
  138.9 4.1 %gather_fusion.2 = f32[1536,3]{1,0:T(8,128)S(1)} fusion(f32[3,3457]{0,1:T(8,128)} %pad_add_fusion, s32[2048]{0:T(1024)S(1)} %copy-done.12), kind=kCustom, calls=%fused_computation.2 | custom fusion | bytes 43008 | tf_op jit(solution)/shard_map/jit(_take)/gather | solution.py:216
  143.5 1.1 copy.275
  144.6 1.1 copy.274
  145.7 1.1 copy.277
  146.8 1.5 bitcast_add_fusion
  148.4 1.9 collective-permute-start.14
  150.3 3.4 %collective-permute-start.15 = (f32[1,3,3,128]{2,3,1,0:T(8,128)S(1)}, f32[1,3,3,128]{2,3,1,0:T(8,128)S(1)}, u32[]{:S(2)}, u32[]{:S(2)}) collective-permute-start(f32[1,3,3,128]{2,3,1,0:T(8,128)S(1)} %get-tuple-element.111), channel_id=1, source_target_pairs={{4,0},{8,4},{12,8},{16,12},{20,16},{24,20},{28,24},{5,1},{9,5},{13... | collective-permute-start | bytes 13832 | tf_op jit(solution)/shard_map/ppermute | solution.py:49
  153.7 1.4 collective-permute-done.14
  155.1 3.7 %collective-permute-done.15 = f32[1,3,3,128]{2,3,1,0:T(8,128)S(1)} collective-permute-done((f32[1,3,3,128]{2,3,1,0:T(8,128)S(1)}, f32[1,3,3,128]{2,3,1,0:T(8,128)S(1)}, u32[]{:S(2)}, u32[]{:S(2)}) %collective-permute-start.15) | collective-permute-done | bytes 4640 | tf_op jit(solution)/shard_map/ppermute | solution.py:49
  158.9 5.3 %collective-permute-start.16 = (f32[1,3,128]{1,2,0:T(8,128)S(1)}, f32[1,3,128]{1,2,0:T(8,128)S(1)}, u32[]{:S(2)}, u32[]{:S(2)}) collective-permute-start(f32[1,3,128]{1,2,0:T(8,128)S(1)} %get-tuple-element.112), channel_id=1, source_target_pairs={{0,1},{1,2},{2,3},{4,5},{5,6},{6,7},{8,9},{9,10},{10,11},{12,13},{... | collective-permute-start | bytes 4616 | tf_op jit(solution)/shard_map/ppermute | solution.py:48
  164.2 1.9 collective-permute-start.17
  166.7 4.6 %collective-permute-done.17 = f32[1,3,128]{1,2,0:T(8,128)S(1)} collective-permute-done((f32[1,3,128]{1,2,0:T(8,128)S(1)}, f32[1,3,128]{1,2,0:T(8,128)S(1)}, u32[]{:S(2)}, u32[]{:S(2)}) %collective-permute-start.17) | collective-permute-done | bytes 1568 | tf_op jit(solution)/shard_map/ppermute | solution.py:49
  171.9 3.3 %collective-permute-start.18 = (f32[1,3,3,6,128]{4,3,2,1,0:T(8,128)S(1)}, f32[1,3,3,6,128]{4,3,2,1,0:T(8,128)S(1)}, u32[]{:S(2)}, u32[]{:S(2)}) collective-permute-start(f32[1,3,3,6,128]{4,3,2,1,0:T(8,128)S(1)} %bitcast.442), channel_id=1, source_target_pairs={{0,32},{32,64},{64,96},{1,33},{33,65},{65,97},{2,34},{34,66},{66,9... | collective-permute-start | bytes 82952 | tf_op jit(solution)/shard_map/ppermute | solution.py:48
  175.3 2.1 collective-permute-start.19
  178.0 1.9 collective-permute-done.19
  180.0 1.9 collective-permute-start.20
  181.9 3.4 %collective-permute-start.21 = (f32[1,3,6,128]{3,2,1,0:T(8,128)S(1)}, f32[1,3,6,128]{3,2,1,0:T(8,128)S(1)}, u32[]{:S(2)}, u32[]{:S(2)}) collective-permute-start(f32[1,3,6,128]{3,2,1,0:T(8,128)S(1)} %get-tuple-element.141), channel_id=1, source_target_pairs={{4,0},{8,4},{12,8},{16,12},{20,16},{24,20},{28,24},{5,1},{9,5},{13... | collective-permute-start | bytes 27656 | tf_op jit(solution)/shard_map/ppermute | solution.py:49
  185.3 2.9 %collective-permute-start.6 = (f32[10,1,16,128]{3,2,1,0:T(8,128)S(1)}, f32[10,1,16,128]{3,2,1,0:T(8,128)S(1)}, u32[]{:S(2)}, u32[]{:S(2)}) collective-permute-start(f32[10,1,16,128]{3,2,1,0:T(8,128)S(1)} %get-tuple-element.109), channel_id=1, source_target_pairs={{0,32},{32,64},{64,96},{1,33},{33,65},{65,97},{2,34},{34,66},{66,9... | collective-permute-start | bytes 245768 | tf_op jit(solution)/shard_map/ppermute | solution.py:48
  188.2 2.4 collective-permute-start.7
  190.7 4.4 %collective-permute-start.22 = (f32[1,6,128]{2,1,0:T(8,128)S(1)}, f32[1,6,128]{2,1,0:T(8,128)S(1)}, u32[]{:S(2)}, u32[]{:S(2)}) collective-permute-start(f32[1,6,128]{2,1,0:T(8,128)S(1)} %get-tuple-element.142), channel_id=1, source_target_pairs={{0,1},{1,2},{2,3},{4,5},{5,6},{6,7},{8,9},{9,10},{10,11},{12,13},{... | collective-permute-start | bytes 9224 | tf_op jit(solution)/shard_map/ppermute | solution.py:48
  195.1 1.9 collective-permute-start.23
  198.7 3.1 %collective-permute-start.8 = (f32[10,8,1,128]{3,2,1,0:T(1,128)S(1)}, f32[10,8,1,128]{3,2,1,0:T(1,128)S(1)}, u32[]{:S(2)}, u32[]{:S(2)}) collective-permute-start(f32[10,8,1,128]{3,2,1,0:T(1,128)S(1)} %get-tuple-element.106), channel_id=1, source_target_pairs={{0,4},{4,8},{8,12},{12,16},{16,20},{20,24},{24,28},{1,5},{5,9},{9,... | collective-permute-start | bytes 122888 | tf_op jit(solution)/shard_map/ppermute | solution.py:48
  201.8 2.1 collective-permute-start.9
  204.6 4.1 %collective-permute-done.9 = f32[10,8,1,128]{3,2,1,0:T(1,128)S(1)} collective-permute-done((f32[10,8,1,128]{3,2,1,0:T(1,128)S(1)}, f32[10,8,1,128]{3,2,1,0:T(1,128)S(1)}, u32[]{:S(2)}, u32[]{:S(2)}) %collective-permute-start.9) | collective-permute-done | bytes 40992 | tf_op jit(solution)/shard_map/ppermute | solution.py:49
  209.0 1.1 fusion.232
  210.1 1.6 copy.265
  211.7 7.2 %collective-permute-start.10 = (f32[10,8,16,1]{2,1,3,0:T(8,128)S(1)}, f32[10,8,16,1]{2,1,3,0:T(8,128)S(1)}, u32[]{:S(2)}, u32[]{:S(2)}) collective-permute-start(f32[10,8,16,1]{2,1,3,0:T(8,128)S(1)} %copy.265), channel_id=1, source_target_pairs={{0,1},{1,2},{2,3},{4,5},{5,6},{6,7},{8,9},{9,10},{10,11},{12,13},{... | collective-permute-start | bytes 15368 | tf_op jit(solution)/shard_map/ppermute | solution.py:48
  219.4 1.9 collective-permute-start.11
  223.4 2.9 %collective-permute-done.11 = f32[10,8,16,1]{2,1,3,0:T(8,128)S(1)} collective-permute-done((f32[10,8,16,1]{2,1,3,0:T(8,128)S(1)}, f32[10,8,16,1]{2,1,3,0:T(8,128)S(1)}, u32[]{:S(2)}, u32[]{:S(2)}) %collective-permute-start.11) | collective-permute-done | bytes 5152 | tf_op jit(solution)/shard_map/ppermute | solution.py:49
  226.3 1.4 copy.268
  227.6 1.7 pad_maximum_fusion
  230.7 0.7 constant_dynamic-update-slice_fusion.105
  235.1 0.7 constant_dynamic-update-slice_fusion.99
  235.8 0.7 constant_dynamic-update-slice_fusion.98
  237.9 0.7 constant_dynamic-update-slice_fusion.95
  (234 shorter events, 27.9 us)
Async XLA Ops:
  0.6 15.5 %copy-start.25 = (f32[19,3,1,1]{0,1,3,2:T(4,128)S(1)}, f32[19,3,1,1]{0,1,3,2:T(4,128)}, u32[]{:S(2)}) copy-start(f32[19,3,1,1]{0,1,3,2:T(4,128)} %constant.234) | copy-start | bytes 688
  0.6 15.5 %copy-start = (f32[19,8,16,128]{3,2,1,0:T(8,128)S(1)}, f32[19,8,16,128]{3,2,1,0:T(8,128)}, u32[]{:S(2)}) copy-start(f32[19,8,16,128]{3,2,1,0:T(8,128)} %param.10) | copy-start | bytes 3735556
  0.7 20.7 %collective-permute-start = (f32[1,1,1,6,128]{4,2,3,1,0:T(1,128)}, f32[1,1,1,6,128]{4,2,3,1,0:T(1,128)S(1)}, u32[]{:S(2)}, u32[]{:S(2)}) collective-permute-start(f32[1,1,1,6,128]{4,2,3,1,0:T(1,128)} %param.14), channel_id=1, source_target_pairs={{0,32},{32,64},{64,96},{1,33},{33,65},{65,97},{2,34},{34,66},{66,9... | collective-permute-start | bytes 9224 | tf_op jit(solution)/shard_map/ppermute | solution.py:48
  4.0 17.4 %collective-permute-start.1 = (f32[1,1,1,6,128]{4,2,3,1,0:T(1,128)}, f32[1,1,1,6,128]{4,2,3,1,0:T(1,128)S(1)}, u32[]{:S(2)}, u32[]{:S(2)}) collective-permute-start(f32[1,1,1,6,128]{4,2,3,1,0:T(1,128)} %param.14), channel_id=1, source_target_pairs={{32,0},{64,32},{96,64},{33,1},{65,33},{97,65},{34,2},{66,34},{98,6... | collective-permute-start | bytes 9224 | tf_op jit(solution)/shard_map/ppermute | solution.py:49
  16.1 1.6 copy-start.4
  16.2 1.6 copy-start.7
  17.8 1.0 copy-start.34
  17.9 3.5 %copy-start.22 = (f32[1,1,1,6,128]{4,2,3,1,0:T(1,128)S(1)}, f32[1,1,1,6,128]{4,2,3,1,0:T(1,128)}, u32[]{:S(2)}) copy-start(f32[1,1,1,6,128]{4,2,3,1,0:T(1,128)} %param.14) | copy-start | bytes 9220
  18.1 1.3 copy-start.1
  21.4 5.9 %collective-permute-start.2 = (f32[3,1,1,6,128]{4,2,3,1,0:T(1,128)S(1)}, f32[3,1,1,6,128]{4,2,3,1,0:T(1,128)S(1)}, u32[]{:S(2)}, u32[]{:S(2)}) collective-permute-start(f32[3,1,1,6,128]{4,2,3,1,0:T(1,128)S(1)} %constant_dynamic-update-slice_fusion.38), channel_id=1, source_target_pairs={{0,4},{4,8},{8,12},{12,16},{16,20},{20,24},{24,28},{1,5},{5,9},{9,... | collective-permute-start | bytes 27656 | tf_op jit(solution)/shard_map/ppermute | solution.py:48
  23.4 6.5 %collective-permute-start.3 = (f32[3,1,1,6,128]{4,2,3,1,0:T(1,128)S(1)}, f32[3,1,1,6,128]{4,2,3,1,0:T(1,128)S(1)}, u32[]{:S(2)}, u32[]{:S(2)}) collective-permute-start(f32[3,1,1,6,128]{4,2,3,1,0:T(1,128)S(1)} %constant_dynamic-update-slice_fusion.38), channel_id=1, source_target_pairs={{4,0},{8,4},{12,8},{16,12},{20,16},{24,20},{28,24},{5,1},{9,5},{13... | collective-permute-start | bytes 27656 | tf_op jit(solution)/shard_map/ppermute | solution.py:49
  29.9 12.0 %collective-permute-start.4 = (f32[3,3,1,6,128]{4,2,3,1,0:T(1,128)S(1)}, f32[3,3,1,6,128]{4,2,3,1,0:T(1,128)S(1)}, u32[]{:S(2)}, u32[]{:S(2)}) collective-permute-start(f32[3,3,1,6,128]{4,2,3,1,0:T(1,128)S(1)} %pad_maximum_fusion.10), channel_id=1, source_target_pairs={{0,1},{1,2},{2,3},{4,5},{5,6},{6,7},{8,9},{9,10},{10,11},{12,13},{... | collective-permute-start | bytes 82952 | tf_op jit(solution)/shard_map/ppermute | solution.py:48
  36.8 6.7 %collective-permute-start.5 = (f32[3,3,1,6,128]{4,2,3,1,0:T(1,128)S(1)}, f32[3,3,1,6,128]{4,2,3,1,0:T(1,128)S(1)}, u32[]{:S(2)}, u32[]{:S(2)}) collective-permute-start(f32[3,3,1,6,128]{4,2,3,1,0:T(1,128)S(1)} %pad_maximum_fusion.10), channel_id=1, source_target_pairs={{1,0},{2,1},{3,2},{5,4},{6,5},{7,6},{9,8},{10,9},{11,10},{13,12},{... | collective-permute-start | bytes 82952 | tf_op jit(solution)/shard_map/ppermute | solution.py:49
  115.1 1.3 copy-start.2
  116.4 0.7 copy-start.26
  118.9 7.5 %copy-start.31 = (s32[1,1,1,256]{3,2,1,0:T(1,128)S(1)}, s32[1,1,1,256]{3,2,1,0:T(1,128)}, u32[]{:S(2)}) copy-start(s32[1,1,1,256]{3,2,1,0:T(1,128)} %param.13) | copy-start | bytes 3076
  118.9 14.1 %copy-start.6 = (f32[3,27,128]{2,0,1:T(4,128)S(1)}, f32[3,27,128]{2,0,1:T(4,128)}, u32[]{:S(2)}) copy-start(f32[3,27,128]{2,0,1:T(4,128)} %get-tuple-element.114) | copy-start | bytes 124420
  127.7 16.9 %collective-permute-start.12 = (f32[1,3,3,3,128]{4,0,3,2,1:T(1,128)S(1)}, f32[1,3,3,3,128]{4,0,3,2,1:T(1,128)S(1)}, u32[]{:S(2)}, u32[]{:S(2)}) collective-permute-start(f32[1,3,3,3,128]{4,0,3,2,1:T(1,128)S(1)} %copy.273), channel_id=1, source_target_pairs={{0,32},{32,64},{64,96},{1,33},{33,65},{65,97},{2,34},{34,66},{66,9... | collective-permute-start | bytes 41480 | tf_op jit(solution)/shard_map/ppermute | solution.py:48
  130.9 14.8 %collective-permute-start.13 = (f32[1,3,3,3,128]{4,0,3,2,1:T(1,128)S(1)}, f32[1,3,3,3,128]{4,0,3,2,1:T(1,128)S(1)}, u32[]{:S(2)}, u32[]{:S(2)}) collective-permute-start(f32[1,3,3,3,128]{4,0,3,2,1:T(1,128)S(1)} %copy.276), channel_id=1, source_target_pairs={{32,0},{64,32},{96,64},{33,1},{65,33},{97,65},{34,2},{66,34},{98,6... | collective-permute-start | bytes 41480 | tf_op jit(solution)/shard_map/ppermute | solution.py:49
  135.5 3.4 %copy-start.12 = (s32[2048]{0:T(1024)S(1)}, s32[2048]{0:T(1024)}, u32[]{:S(2)}) copy-start(s32[2048]{0:T(1024)} %pad_clamp_fusion) | copy-start | bytes 24580
  135.5 7.5 %copy-start.13 = (pred[12,128]{1,0:T(8,128)(4,1)S(1)}, pred[12,128]{1,0:T(8,128)(4,1)}, u32[]{:S(2)}) copy-start(pred[12,128]{1,0:T(8,128)(4,1)} %compare_and_fusion.1) | copy-start | bytes 4612
  146.8 6.9 %copy-start.9 = (s32[1,1,1,12,128]{4,2,3,1,0:T(1,128)S(1)}, s32[1,1,1,12,128]{4,2,3,1,0:T(1,128)}, u32[]{:S(2)}) copy-start(s32[1,1,1,12,128]{4,2,3,1,0:T(1,128)} %param.15) | copy-start | bytes 18436
  148.3 22.9 %copy-start.5 = (f32[1,1,1,3,128]{3,4,2,1,0:T(8,128)S(1)}, f32[1,1,1,3,128]{3,4,2,1,0:T(8,128)}, u32[]{:S(2)}) copy-start(f32[1,1,1,3,128]{3,4,2,1,0:T(8,128)} %copy.290) | copy-start | bytes 4612
  148.3 22.9 %copy-start.33 = (f32[3]{0:T(128)S(1)}, f32[3]{0:T(128)}, u32[]{:S(2)}) copy-start(f32[3]{0:T(128)} %constant.233) | copy-start | bytes 40
  148.4 6.7 %collective-permute-start.14 = (f32[1,3,3,128]{2,3,1,0:T(8,128)S(1)}, f32[1,3,3,128]{2,3,1,0:T(8,128)S(1)}, u32[]{:S(2)}, u32[]{:S(2)}) collective-permute-start(f32[1,3,3,128]{2,3,1,0:T(8,128)S(1)} %get-tuple-element.110), channel_id=1, source_target_pairs={{0,4},{4,8},{8,12},{12,16},{16,20},{20,24},{24,28},{1,5},{5,9},{9,... | collective-permute-start | bytes 13832 | tf_op jit(solution)/shard_map/ppermute | solution.py:48
  150.3 8.5 %collective-permute-start.15 = (f32[1,3,3,128]{2,3,1,0:T(8,128)S(1)}, f32[1,3,3,128]{2,3,1,0:T(8,128)S(1)}, u32[]{:S(2)}, u32[]{:S(2)}) collective-permute-start(f32[1,3,3,128]{2,3,1,0:T(8,128)S(1)} %get-tuple-element.111), channel_id=1, source_target_pairs={{4,0},{8,4},{12,8},{16,12},{20,16},{24,20},{28,24},{5,1},{9,5},{13... | collective-permute-start | bytes 13832 | tf_op jit(solution)/shard_map/ppermute | solution.py:49
  153.7 17.7 %copy-start.24 = (f32[27,3]{0,1:T(4,128)S(1)}, f32[27,3]{0,1:T(4,128)}, u32[]{:S(2)}) copy-start(f32[27,3]{0,1:T(4,128)} %maximum_bitcast_fusion) | copy-start | bytes 976
  153.7 17.8 %copy-start.8 = (f32[27,128]{1,0:T(8,128)S(1)}, f32[27,128]{1,0:T(8,128)}, u32[]{:S(2)}) copy-start(f32[27,128]{1,0:T(8,128)} %fusion.175) | copy-start | bytes 41476
  153.7 17.8 %copy-start.32 = (s32[1,1,1,128]{3,2,1,0:T(1,128)S(1)}, s32[1,1,1,128]{3,2,1,0:T(1,128)}, u32[]{:S(2)}) copy-start(s32[1,1,1,128]{3,2,1,0:T(1,128)} %param.17) | copy-start | bytes 1540
  158.9 7.8 %collective-permute-start.16 = (f32[1,3,128]{1,2,0:T(8,128)S(1)}, f32[1,3,128]{1,2,0:T(8,128)S(1)}, u32[]{:S(2)}, u32[]{:S(2)}) collective-permute-start(f32[1,3,128]{1,2,0:T(8,128)S(1)} %get-tuple-element.112), channel_id=1, source_target_pairs={{0,1},{1,2},{2,3},{4,5},{5,6},{6,7},{8,9},{9,10},{10,11},{12,13},{... | collective-permute-start | bytes 4616 | tf_op jit(solution)/shard_map/ppermute | solution.py:48
  164.2 7.1 %collective-permute-start.17 = (f32[1,3,128]{1,2,0:T(8,128)S(1)}, f32[1,3,128]{1,2,0:T(8,128)S(1)}, u32[]{:S(2)}, u32[]{:S(2)}) collective-permute-start(f32[1,3,128]{1,2,0:T(8,128)S(1)} %get-tuple-element.113), channel_id=1, source_target_pairs={{1,0},{2,1},{3,2},{5,4},{6,5},{7,6},{9,8},{10,9},{11,10},{13,12},{... | collective-permute-start | bytes 4616 | tf_op jit(solution)/shard_map/ppermute | solution.py:49
  171.9 25.2 %copy-start.3 = (f32[10,8,16,128]{3,2,1,0:T(8,128)S(1)}, f32[10,8,16,128]{3,2,1,0:T(8,128)}, u32[]{:S(2)}) copy-start(f32[10,8,16,128]{3,2,1,0:T(8,128)} %get-tuple-element.82) | copy-start | bytes 1966084
  171.9 6.1 %collective-permute-start.18 = (f32[1,3,3,6,128]{4,3,2,1,0:T(8,128)S(1)}, f32[1,3,3,6,128]{4,3,2,1,0:T(8,128)S(1)}, u32[]{:S(2)}, u32[]{:S(2)}) collective-permute-start(f32[1,3,3,6,128]{4,3,2,1,0:T(8,128)S(1)} %bitcast.442), channel_id=1, source_target_pairs={{0,32},{32,64},{64,96},{1,33},{33,65},{65,97},{2,34},{34,66},{66,9... | collective-permute-start | bytes 82952 | tf_op jit(solution)/shard_map/ppermute | solution.py:48
  175.3 4.7 %collective-permute-start.19 = (f32[1,3,3,6,128]{4,3,2,1,0:T(8,128)S(1)}, f32[1,3,3,6,128]{4,3,2,1,0:T(8,128)S(1)}, u32[]{:S(2)}, u32[]{:S(2)}) collective-permute-start(f32[1,3,3,6,128]{4,3,2,1,0:T(8,128)S(1)} %bitcast.443), channel_id=1, source_target_pairs={{32,0},{64,32},{96,64},{33,1},{65,33},{97,65},{34,2},{66,34},{98,6... | collective-permute-start | bytes 82952 | tf_op jit(solution)/shard_map/ppermute | solution.py:49
  180.0 10.7 %collective-permute-start.20 = (f32[1,3,6,128]{3,2,1,0:T(8,128)S(1)}, f32[1,3,6,128]{3,2,1,0:T(8,128)S(1)}, u32[]{:S(2)}, u32[]{:S(2)}) collective-permute-start(f32[1,3,6,128]{3,2,1,0:T(8,128)S(1)} %get-tuple-element.140), channel_id=1, source_target_pairs={{0,4},{4,8},{8,12},{12,16},{16,20},{20,24},{24,28},{1,5},{5,9},{9,... | collective-permute-start | bytes 27656 | tf_op jit(solution)/shard_map/ppermute | solution.py:48
  181.9 8.7 %collective-permute-start.21 = (f32[1,3,6,128]{3,2,1,0:T(8,128)S(1)}, f32[1,3,6,128]{3,2,1,0:T(8,128)S(1)}, u32[]{:S(2)}, u32[]{:S(2)}) collective-permute-start(f32[1,3,6,128]{3,2,1,0:T(8,128)S(1)} %get-tuple-element.141), channel_id=1, source_target_pairs={{4,0},{8,4},{12,8},{16,12},{20,16},{24,20},{28,24},{5,1},{9,5},{13... | collective-permute-start | bytes 27656 | tf_op jit(solution)/shard_map/ppermute | solution.py:49
  185.3 11.8 %copy-start.10 = (pred[128]{0:T(512)(128)(4,1)S(1)}, pred[128]{0:T(512)(128)(4,1)}, u32[]{:S(2)}) copy-start(pred[128]{0:T(512)(128)(4,1)} %get-tuple-element.165) | copy-start | bytes 388
  185.3 11.8 %copy-start.11 = (pred[128]{0:T(512)(128)(4,1)S(1)}, pred[128]{0:T(512)(128)(4,1)}, u32[]{:S(2)}) copy-start(pred[128]{0:T(512)(128)(4,1)} %get-tuple-element.166) | copy-start | bytes 388
  185.3 11.8 %copy-start.17 = (pred[8,16]{1,0:T(8,128)(4,1)S(1)}, pred[8,16]{1,0:T(8,128)(4,1)}, u32[]{:S(2)}) copy-start(pred[8,16]{1,0:T(8,128)(4,1)} %get-tuple-element.157) | copy-start | bytes 388
  185.3 11.7 %collective-permute-start.6 = (f32[10,1,16,128]{3,2,1,0:T(8,128)S(1)}, f32[10,1,16,128]{3,2,1,0:T(8,128)S(1)}, u32[]{:S(2)}, u32[]{:S(2)}) collective-permute-start(f32[10,1,16,128]{3,2,1,0:T(8,128)S(1)} %get-tuple-element.109), channel_id=1, source_target_pairs={{0,32},{32,64},{64,96},{1,33},{33,65},{65,97},{2,34},{34,66},{66,9... | collective-permute-start | bytes 245768 | tf_op jit(solution)/shard_map/ppermute | solution.py:48
  188.2 8.8 %collective-permute-start.7 = (f32[10,1,16,128]{3,2,1,0:T(8,128)S(1)}, f32[10,1,16,128]{3,2,1,0:T(8,128)S(1)}, u32[]{:S(2)}, u32[]{:S(2)}) collective-permute-start(f32[10,1,16,128]{3,2,1,0:T(8,128)S(1)} %get-tuple-element.108), channel_id=1, source_target_pairs={{32,0},{64,32},{96,64},{33,1},{65,33},{97,65},{34,2},{66,34},{98,6... | collective-permute-start | bytes 245768 | tf_op jit(solution)/shard_map/ppermute | solution.py:49
  190.7 13.3 %collective-permute-start.22 = (f32[1,6,128]{2,1,0:T(8,128)S(1)}, f32[1,6,128]{2,1,0:T(8,128)S(1)}, u32[]{:S(2)}, u32[]{:S(2)}) collective-permute-start(f32[1,6,128]{2,1,0:T(8,128)S(1)} %get-tuple-element.142), channel_id=1, source_target_pairs={{0,1},{1,2},{2,3},{4,5},{5,6},{6,7},{8,9},{9,10},{10,11},{12,13},{... | collective-permute-start | bytes 9224 | tf_op jit(solution)/shard_map/ppermute | solution.py:48
  195.1 8.9 %collective-permute-start.23 = (f32[1,6,128]{2,1,0:T(8,128)S(1)}, f32[1,6,128]{2,1,0:T(8,128)S(1)}, u32[]{:S(2)}, u32[]{:S(2)}) collective-permute-start(f32[1,6,128]{2,1,0:T(8,128)S(1)} %get-tuple-element.143), channel_id=1, source_target_pairs={{1,0},{2,1},{3,2},{5,4},{6,5},{7,6},{9,8},{10,9},{11,10},{13,12},{... | collective-permute-start | bytes 9224 | tf_op jit(solution)/shard_map/ppermute | solution.py:49
  197.0 0.8 copy-start.16
  198.7 5.9 %collective-permute-start.8 = (f32[10,8,1,128]{3,2,1,0:T(1,128)S(1)}, f32[10,8,1,128]{3,2,1,0:T(1,128)S(1)}, u32[]{:S(2)}, u32[]{:S(2)}) collective-permute-start(f32[10,8,1,128]{3,2,1,0:T(1,128)S(1)} %get-tuple-element.106), channel_id=1, source_target_pairs={{0,4},{4,8},{8,12},{12,16},{16,20},{20,24},{24,28},{1,5},{5,9},{9,... | collective-permute-start | bytes 122888 | tf_op jit(solution)/shard_map/ppermute | solution.py:48
  201.8 6.9 %collective-permute-start.9 = (f32[10,8,1,128]{3,2,1,0:T(1,128)S(1)}, f32[10,8,1,128]{3,2,1,0:T(1,128)S(1)}, u32[]{:S(2)}, u32[]{:S(2)}) collective-permute-start(f32[10,8,1,128]{3,2,1,0:T(1,128)S(1)} %get-tuple-element.107), channel_id=1, source_target_pairs={{4,0},{8,4},{12,8},{16,12},{20,16},{24,20},{28,24},{5,1},{9,5},{13... | collective-permute-start | bytes 122888 | tf_op jit(solution)/shard_map/ppermute | solution.py:49
  210.1 11.3 %copy-start.15 = (pred[8,16]{1,0:T(8,128)(4,1)S(1)}, pred[8,16]{1,0:T(8,128)(4,1)}, u32[]{:S(2)}) copy-start(pred[8,16]{1,0:T(8,128)(4,1)} %get-tuple-element.161) | copy-start | bytes 388
  210.1 12.0 %copy-start.14 = (pred[8,16]{1,0:T(8,128)(4,1)S(1)}, pred[8,16]{1,0:T(8,128)(4,1)}, u32[]{:S(2)}) copy-start(pred[8,16]{1,0:T(8,128)(4,1)} %get-tuple-element.158) | copy-start | bytes 388
  211.7 11.1 %collective-permute-start.10 = (f32[10,8,16,1]{2,1,3,0:T(8,128)S(1)}, f32[10,8,16,1]{2,1,3,0:T(8,128)S(1)}, u32[]{:S(2)}, u32[]{:S(2)}) collective-permute-start(f32[10,8,16,1]{2,1,3,0:T(8,128)S(1)} %copy.265), channel_id=1, source_target_pairs={{0,1},{1,2},{2,3},{4,5},{5,6},{6,7},{8,9},{9,10},{10,11},{12,13},{... | collective-permute-start | bytes 15368 | tf_op jit(solution)/shard_map/ppermute | solution.py:48
  219.4 6.8 %collective-permute-start.11 = (f32[10,8,16,1]{2,1,3,0:T(8,128)S(1)}, f32[10,8,16,1]{2,1,3,0:T(8,128)S(1)}, u32[]{:S(2)}, u32[]{:S(2)}) collective-permute-start(f32[10,8,16,1]{2,1,3,0:T(8,128)S(1)} %copy.266), channel_id=1, source_target_pairs={{1,0},{2,1},{3,2},{5,4},{6,5},{7,6},{9,8},{10,9},{11,10},{13,12},{... | collective-permute-start | bytes 15368 | tf_op jit(solution)/shard_map/ppermute | solution.py:49
  229.3 0.7 copy-start.18
  229.3 0.7 copy-start.19
  229.3 0.7 copy-start.23
  229.3 1.4 copy-start.20
  229.3 1.4 copy-start.21
  229.4 2.1 copy-start.30
  229.4 2.8 %copy-start.29 = (pred[8,16]{1,0:T(8,128)(4,1)S(1)}, pred[8,16]{1,0:T(8,128)(4,1)}, u32[]{:S(2)}) copy-start(pred[8,16]{1,0:T(8,128)(4,1)} %get-tuple-element.162) | copy-start | bytes 388
  229.4 3.5 %copy-start.28 = (pred[8,16]{1,0:T(8,128)(4,1)S(1)}, pred[8,16]{1,0:T(8,128)(4,1)}, u32[]{:S(2)}) copy-start(pred[8,16]{1,0:T(8,128)(4,1)} %get-tuple-element.163) | copy-start | bytes 388
  229.4 4.2 %copy-start.27 = (pred[8,16]{1,0:T(8,128)(4,1)S(1)}, pred[8,16]{1,0:T(8,128)(4,1)}, u32[]{:S(2)}) copy-start(pred[8,16]{1,0:T(8,128)(4,1)} %get-tuple-element.159) | copy-start | bytes 388
where the time goes:
time: 243 us; the launch traced here: 240 us
  local copies, waits for them, and re-layouts  92 us (38%)
  starting transfers between devices  74 us (30%)
  other arithmetic  36.9 us (15%)
  waiting for transfers between devices  22.7 us (9%)
  matrix products  12.4 us (5%)
    gather x2, local copies, waits for them, and re-layouts, body(): solid_velocity = SPEED_UNIT * jnp.take(touch_velocity, intersection, axis=1)  65.4 us
    ppermute x12, starting transfers between devices, padded(): before = lax.ppermute(last, axis, up)  45.5 us
    ppermute x12, starting transfers between devices, padded(): after = lax.ppermute(first, axis, down)  28.5 us
    ppermute x12, waiting for transfers between devices, padded(): after = lax.ppermute(first, axis, down)  21.4 us
    unnamed x37, other arithmetic  13.3 us
    dot_general x1, matrix products, add_block(): jnp.einsum('dc,kc->dk', block_force, onehot, precision=lax.Precision.HIGH...  7.43 us
    unnamed x116, local copies, waits for them, and re-layouts  5.72 us
  transfers between devices with their start and end apart: 24, of which 8 were waited for; matrix products, arithmetic and copies ran while one was open for 16% of the time, Pallas kernels for 0%

commit v1 on v0

v1 whole, which is shorter than its diff:
```python
import jax
import jax.numpy as jnp
from jax import lax
from jax.experimental import pallas as pl
from jax.experimental.pallas import tpu as pltpu
from jax.sharding import PartitionSpec as P

LATTICE = [
    (0, 0, 0),
    (1, 0, 0),
    (-1, 0, 0),
    (0, 1, 0),
    (0, -1, 0),
    (0, 0, 1),
    (0, 0, -1),
    (1, 1, 0),
    (-1, -1, 0),
    (1, -1, 0),
    (-1, 1, 0),
    (1, 0, 1),
    (-1, 0, -1),
    (1, 0, -1),
    (-1, 0, 1),
    (0, 1, 1),
    (0, -1, -1),
    (0, 1, -1),
    (0, -1, 1),
]
OPPOSITE = [0, 2, 1, 4, 3, 6, 5, 8, 7, 10, 9, 12, 11, 14, 13, 16, 15, 18, 17]
WEIGHTS = [1.0 / 3.0] + [1.0 / 18.0] * 6 + [1.0 / 36.0] * 12
PAIRS = [(i, i + 1) for i in range(1, 19, 2)]
RELAX_TIME = 0.8
SPEED_UNIT = 0.05
FORCE_SCALE = 0.1
CONTACT_GAIN = 1.0
GRAVITY_STEP = 0.1
R = 8.0
CX, CY, CZ, SLOTS, TOUCHES, CANDIDATES = 8, 16, 128, 128, 256, 12
SPANS = (CX / R, CY / R, CZ / R)
AXES = ("gx", "gy", "gz")
MESH = pl.DeviceIdType.MESH

X_UP, X_DOWN = [1, 7, 9, 11, 13], [2, 8, 10, 12, 14]
Y_MOVERS = [[3, 7, 10, 15, 17], [4, 9, 8, 18, 16]]
Z_MOVERS = [[5, 11, 14, 15, 18], [6, 13, 12, 17, 16]]
PLACE = {d: n for n, d in enumerate(X_UP + X_DOWN + [0, 3, 4, 5, 6, 15, 16, 17, 18])}
MOVE_CODES = [4, 10, 12, 13, 14, 16, 22]
PAD = 8


def offset_of(code):
    return (code // 9 - 1, code // 3 % 3 - 1, code % 3 - 1)


def lane_gather(table, index):
    return jnp.take_along_axis(table, index, axis=1, mode="promise_in_bounds")


def dot_lanes(a, b):
    return lax.dot_general(a, b, (((1,), (1,)), ((), ())), preferred_element_type=jnp.float32)


def kernel(
    sizes,
    pop,
    frac,
    inter,
    touch,
    part,
    cont,
    dcode,
    dslot,
    out_pop,
    out_part,
    f_v,
    frac_v,
    int_v,
    touch_v,
    cont_v,
    dcode_v,
    dslot_v,
    nb,
    mac,
    split,
    inv_v,
    inv2_v,
    cs,
    cr,
    rel,
    ys,
    yr,
    ye,
    zm,
    zs,
    zr,
    ze,
    rec,
    ds,
    dr,
    in_sem,
    pop_sem,
    a_send,
    a_recv,
    b_send,
    b_recv,
    c_send,
    c_recv,
    d_send,
    d_recv,
):
    here = [lax.axis_index(axis) for axis in AXES]

    def device(offset):
        return tuple(
            here[n] if offset[n] == 0 else lax.rem(here[n] + offset[n] + sizes[n], sizes[n])
            for n in range(3)
        )

    def exists(offset):
        ok = None
        for n in range(3):
            if isinstance(offset[n], int) and offset[n] == 0:
                continue
            there = here[n] + offset[n]
            test = (there >= 0) & (there < sizes[n])
            ok = test if ok is None else ok & test
        return ok

    others = [code for code in range(27) if code != 13]

    barrier = pltpu.get_barrier_semaphore()
    for code in others:
        pl.semaphore_signal(
            barrier, inc=1, device_id=device(offset_of(code)), device_id_type=MESH
        )

    small = [
        (part.at[0, 0, 0], nb.at[13, pl.ds(0, 6)]),
        (touch.at[0, 0], touch_v),
        (dcode.at[0, 0], dcode_v),
        (dslot.at[0, 0], dslot_v),
        (frac, frac_v),
        (inter, int_v),
        (cont.at[0, 0, 0], cont_v),
    ]
    loads = [pltpu.make_async_copy(s, d, in_sem.at[n]) for n, (s, d) in enumerate(small)]
    for load in loads:
        load.start()

    def pop_load(x):
        return pltpu.make_async_copy(pop.at[:, x], f_v.at[:, x], pop_sem.at[x])

    for x in range(CX):
        pop_load(x).start()

    lane = lax.broadcasted_iota(jnp.int32, (8, 128), 1)
    sub = lax.broadcasted_iota(jnp.int32, (8, 128), 0)

    loads[1].wait()
    loads[2].wait()
    loads[3].wait()
    entry = touch_v[0:1, :]
    wide = lax.broadcasted_iota(jnp.int32, (112, TOUCHES), 1)
    row = lax.broadcasted_iota(jnp.int32, (112, TOUCHES), 0)
    named = jnp.where((entry >> 7) == (row >> 2), wide + 1, 0).astype(jnp.float32)
    slot_row = lax.broadcasted_iota(jnp.int32, (SLOTS, TOUCHES), 0)
    placed = jnp.where((entry & 127) == slot_row, 1.0, 0.0)
    inverse = dot_lanes(named.astype(jnp.bfloat16), placed.astype(jnp.bfloat16))
    inv_v[...] = (inverse.astype(jnp.int32) - 1).reshape(14, 8, 128)
    code_row = jnp.broadcast_to(dcode_v[0:1, :], (8, 128))
    moved = jnp.concatenate(
        [jnp.where(code_row == code, lane + 1, 0).astype(jnp.float32) for code in MOVE_CODES]
        + [jnp.zeros((8, 128), jnp.float32)],
        axis=0,
    )
    tall = lax.broadcasted_iota(jnp.int32, (SLOTS, SLOTS), 0)
    landing = jnp.where(dslot_v[0:1, :] == tall, 1.0, 0.0)
    inverse2 = dot_lanes(moved.astype(jnp.bfloat16), landing.astype(jnp.bfloat16))
    inv2_v[...] = (inverse2.astype(jnp.int32) - 1).reshape(8, 8, 128)

    loads[0].wait()
    pl.semaphore_wait(barrier, 26)

    def send_a(code):
        return pltpu.make_async_remote_copy(
            src_ref=nb.at[13],
            dst_ref=nb.at[26 - code],
            send_sem=a_send.at[code],
            recv_sem=a_recv.at[26 - code],
            device_id=device(offset_of(code)),
            device_id_type=MESH,
        )

    for code in others:
        send_a(code).start()

    loads[4].wait()
    loads[5].wait()

    def moments(x, carry):
        pop_load(x).wait()
        for half in range(2):
            rows = pl.ds(8 * half, 8)
            f = [f_v[d, x, rows, :] for d in range(19)]
            rho = f[0]
            momentum = [None, None, None]
            for d in range(1, 19):
                rho = rho + f[d]
            for n in range(3):
                for d in range(1, 19):
                    if LATTICE[d][n] == 1:
                        momentum[n] = f[d] if momentum[n] is None else momentum[n] + f[d]
                for d in range(1, 19):
                    if LATTICE[d][n] == -1:
                        momentum[n] = momentum[n] - f[d]
            eps = frac_v[x, rows, :]
            weight = jnp.where(
                int_v[x, rows, :] < TOUCHES,
                eps * (RELAX_TIME - 0.5) / (1.0 - eps + (RELAX_TIME - 0.5)),
                0.0,
            )
            scale = 1.0 / rho
            mac[0, x, rows, :] = rho
            mac[1, x, rows, :] = weight
            for n in range(3):
                mac[2 + n, x, rows, :] = momentum[n] * scale
            for n, term in enumerate(momentum + [rho]):
                term = term * weight
                high = term.astype(jnp.bfloat16).astype(jnp.float32)
                start = 8 * (CY * x + 8 * half)
                split[pl.ds(start + n, 8, stride=8), :] = high
                split[pl.ds(start + 4 + n, 8, stride=8), :] = term - high
        return carry

    lax.fori_loop(0, CX, moments, 0)

    low_row = lax.broadcasted_iota(jnp.int32, (32, 128), 0)

    def add_slab(x, total):
        left, right = [], []
        for y in range(CY):
            slots = int_v[x, pl.ds(y, 1), :]
            tile = split[pl.ds(pl.multiple_of(8 * (CY * x + y), 8), 8), :]
            upper = jnp.broadcast_to(slots >> 5, (8, 128))
            picked = [jnp.where(upper == a, tile, 0.0) for a in range(8)]
            left.append(jnp.concatenate(picked, axis=0).astype(jnp.bfloat16))
            lower = jnp.broadcast_to(slots & 31, (32, 128))
            right.append(jnp.where(lower == low_row, 1.0, 0.0).astype(jnp.bfloat16))
        return total + dot_lanes(
            jnp.concatenate(left, axis=1), jnp.concatenate(right, axis=1)
        )

    total = lax.fori_loop(0, CX, add_slab, jnp.zeros((64, 32), jnp.float32))
    tables = []
    for h in range(2):
        table = jnp.concatenate(
            [total[8 * a : 8 * a + 8, :] for a in range(4 * h, 4 * h + 4)], axis=1
        )
        tables.append(table + pltpu.roll(table, 4, 0))

    for q in range(14):
        source = inv_v[q]
        index = source & 127
        picked = jnp.where(
            source < 128, lane_gather(tables[0], index), lane_gather(tables[1], index)
        )
        picked = jnp.where(source >= 0, picked, 0.0)
        cs[2 * q] = picked[0:4, :]
        cs[2 * q + 1] = picked[4:8, :]

    def send_c(code):
        return pltpu.make_async_remote_copy(
            src_ref=cs.at[code],
            dst_ref=cr.at[26 - code],
            send_sem=c_send.at[code],
            recv_sem=c_recv.at[26 - code],
            device_id=device(offset_of(code)),
            device_id_type=MESH,
        )

    for code in others:
        send_c(code).start()

    def relax(x, carry):
        for half in range(2):
            rows = pl.ds(8 * half, 8)
            dest = pl.ds(PAD + 8 * half, 8)
            rho = mac[0, x, rows, :]
            weight = mac[1, x, rows, :]
            u = [mac[2 + n, x, rows, :] for n in range(3)]
            alpha = (1.0 - weight) * (1.0 / RELAX_TIME)
            keep = 1.0 - alpha - weight
            even = (alpha - weight) * rho
            odd = 3.0 * (alpha + weight) * rho
            base = even * (1.0 - 1.5 * (u[0] * u[0] + u[1] * u[1] + u[2] * u[2]))
            even = 4.5 * even
            rel[PLACE[0], x + 1, dest, :] = (1.0 - alpha) * f_v[0, x, rows, :] + WEIGHTS[0] * base
            for i, j in PAIRS:
                along = None
                for n in range(3):
                    if LATTICE[i][n] == 1:
                        along = u[n] if along is None else along + u[n]
                    elif LATTICE[i][n] == -1:
                        along = -u[n] if along is None else along - u[n]
                symmetric = WEIGHTS[i] * (base + even * along * along)
                skew = WEIGHTS[i] * (odd * along)
                fi, fj = f_v[i, x, rows, :], f_v[j, x, rows, :]
                rel[PLACE[i], x + 1, dest, :] = keep * fi + weight * fj + (symmetric + skew)
                rel[PLACE[j], x + 1, dest, :] = keep * fj + weight * fi + (symmetric - skew)
        return carry

    lax.fori_loop(0, CX, relax, 0)

    for code in others:
        send_a(code).wait()

    def mask_records(code, carry):
        ok = exists((code // 9 - 1, code // 3 % 3 - 1, code % 3 - 1))
        nb[code] = jnp.where(ok, nb[code], 0.0)
        return carry

    lax.fori_loop(0, 27, mask_records, 0)

    touch_code = [jnp.broadcast_to(touch_v[0:1, pl.ds(128 * h, 128)] >> 7, (8, 128)) for h in range(2)]
    touch_slot = [jnp.broadcast_to(touch_v[0:1, pl.ds(128 * h, 128)] & 127, (8, 128)) for h in range(2)]

    def find_velocity(code, found):
        tile = nb[code]
        return tuple(
            jnp.where(touch_code[h] == code, lane_gather(tile, touch_slot[h]), found[h])
            for h in range(2)
        )

    zero = jnp.zeros((8, 128), jnp.float32)
    found = lax.fori_loop(0, 27, find_velocity, (zero, zero))
    speed = [
        [jnp.broadcast_to(SPEED_UNIT * found[h][3 + n : 4 + n, :], (8, 128)) for n in range(3)]
        for h in range(2)
    ]

    def solid(x, carry):
        for half in range(2):
            rows = pl.ds(8 * half, 8)
            dest = pl.ds(PAD + 8 * half, 8)
            slots = int_v[x, rows, :]
            index = slots & 127
            first = slots < 128
            v = [
                jnp.where(first, lane_gather(speed[0][n], index), lane_gather(speed[1][n], index))
                for n in range(3)
            ]
            mass = mac[0, x, rows, :] * mac[1, x, rows, :]
            base = mass * (1.0 - 1.5 * (v[0] * v[0] + v[1] * v[1] + v[2] * v[2]))
            even = 4.5 * mass
            odd = 3.0 * mass
            relaxed = {}
            relaxed[0] = rel[PLACE[0], x + 1, dest, :] + WEIGHTS[0] * base
            for i, j in PAIRS:
                along = None
                for n in range(3):
                    if LATTICE[i][n] == 1:
                        along = v[n] if along is None else along + v[n]
                    elif LATTICE[i][n] == -1:
                        along = -v[n] if along is None else along - v[n]
                symmetric = WEIGHTS[i] * (base + even * along * along)
                skew = WEIGHTS[i] * (odd * along)
                relaxed[i] = rel[PLACE[i], x + 1, dest, :] + (symmetric + skew)
                relaxed[j] = rel[PLACE[j], x + 1, dest, :] + (symmetric - skew)
            for d in range(19):
                rel[PLACE[d], x + 1, dest, :] = relaxed[d]
            packed = zero
            for side in range(2):
                edge = 127 if side == 0 else 0
                for n, d in enumerate(Z_MOVERS[side]):
                    packed = jnp.where(
                        lane == 8 * side + n, relaxed[d][:, edge : edge + 1], packed
                    )
            zm[pl.ds(pl.multiple_of(CY * x + 8 * half, 8), 8), :] = packed
            side = 1 - half
            edge = 7 if side == 0 else 0
            for n, d in enumerate(Y_MOVERS[side]):
                target = lax.rem(x + LATTICE[d][0] + CX, CX)
                ys[side, n, pl.ds(target, 1), :] = relaxed[d][edge : edge + 1, :]
        return carry

    lax.fori_loop(0, CX, solid, 0)

    across = jnp.transpose(zm[...])
    for side in range(2):
        tile = across[8 * side : 8 * side + 8, :]
        up_y = jnp.where((lane & 15) == 0, pltpu.roll(tile, 128 - 15, 1), pltpu.roll(tile, 1, 1))
        down_y = jnp.where((lane & 15) == 15, pltpu.roll(tile, 15, 1), pltpu.roll(tile, 127, 1))
        tile = jnp.where(sub == 1, pltpu.roll(tile, 16, 1), tile)
        tile = jnp.where(sub == 2, pltpu.roll(tile, 112, 1), tile)
        tile = jnp.where(sub == 3, up_y, tile)
        zs[side] = jnp.where(sub == 4, down_y, tile)

    body_rows = pl.ds(PAD, CY)
    moves = [
        (rel.at[pl.ds(0, 5), CX, body_rows], rel.at[pl.ds(0, 5), 0, body_rows], (1, 0, 0)),
        (rel.at[pl.ds(5, 5), 1, body_rows], rel.at[pl.ds(5, 5), CX + 1, body_rows], (-1, 0, 0)),
    ]
    for side in range(2):
        step = 1 - 2 * side
        moves.append((ys.at[side], yr.at[side], (0, step, 0)))
        moves.append((ys.at[side, 1], ye.at[side, 0], (1, step, 0)))
        moves.append((ys.at[side, 2], ye.at[side, 1], (-1, step, 0)))
        moves.append((zs.at[side], zr.at[side], (0, 0, step)))
        moves.append((zs.at[side], ze.at[side, 0], (1, 0, step)))
        moves.append((zs.at[side], ze.at[side, 1], (-1, 0, step)))
        moves.append((zs.at[side], ze.at[side, 2], (0, 1, step)))
        moves.append((zs.at[side], ze.at[side, 3], (0, -1, step)))
    b_copies = [
        pltpu.make_async_remote_copy(
            src_ref=source,
            dst_ref=target,
            send_sem=b_send.at[n],
            recv_sem=b_recv.at[n],
            device_id=device(offset),
            device_id_type=MESH,
        )
        for n, (source, target, offset) in enumerate(moves)
    ]
    for copy in b_copies:
        copy.start()

    loads[6].wait()
    listed = [
        cont_v[0:8, :],
        jnp.concatenate([cont_v[8:12, :], jnp.full((4, 128), 27 * SLOTS, jnp.int32)], axis=0),
    ]
    listed_code = [entries >> 7 for entries in listed]
    listed_slot = [entries & 127 for entries in listed]

    def find_partner(code, partner):
        shifts = (code // 9 - 1, code // 3 % 3 - 1, code % 3 - 1)
        result = []
        for n in range(3):
            line = nb[code, pl.ds(n, 1), :] + shifts[n].astype(jnp.float32) * SPANS[n]
            line = jnp.broadcast_to(line, (8, 128))
            for h in range(2):
                result.append(
                    jnp.where(
                        listed_code[h] == code,
                        lane_gather(line, listed_slot[h]),
                        partner[2 * n + h],
                    )
                )
        return tuple(result)

    partner = lax.fori_loop(0, 27, find_partner, (zero,) * 6)
    force = [None, None, None]
    for h in range(2):
        apart = [nb[13, n : n + 1, :] - partner[2 * n + h] for n in range(3)]
        square = apart[0] * apart[0] + apart[1] * apart[1] + apart[2] * apart[2]
        soften = 1.0 + 0.25 * square
        strength = jnp.where(listed_code[h] < 27, CONTACT_GAIN / (soften * soften), 0.0)
        for n in range(3):
            term = jnp.sum(apart[n] * strength, axis=0, keepdims=True)
            force[n] = term if h == 0 else force[n] + term

    for code in others:
        send_c(code).wait()
    hydro = cs[13]
    for code in others:
        hydro = hydro + jnp.where(exists(offset_of(code)), cr[code], 0.0)
    rec[6:8, :] = jnp.zeros((2, 128), jnp.float32)
    for n in range(3):
        speed_old = nb[13, 3 + n : 4 + n, :]
        pulled = hydro[n : n + 1, :] - (SPEED_UNIT * speed_old) * hydro[3:4, :]
        speed_new = speed_old + FORCE_SCALE * pulled + force[n]
        if n == 2:
            speed_new = speed_new - GRAVITY_STEP
        rec[3 + n : 4 + n, :] = speed_new
        rec[n : n + 1, :] = nb[13, n : n + 1, :] + speed_new * (SPEED_UNIT / R)

    record = rec[...]
    for n, code in enumerate(MOVE_CODES):
        shift = zero
        for axis, step in enumerate(offset_of(code)):
            if step != 0:
                shift = jnp.where(sub == axis, step * SPANS[axis], shift)
        source = inv2_v[n]
        picked = lane_gather(record - shift, source & 127)
        ds[n] = jnp.where(source >= 0, picked, 0.0)
    d_copies = [
        pltpu.make_async_remote_copy(
            src_ref=ds.at[n],
            dst_ref=dr.at[6 - n],
            send_sem=d_send.at[n],
            recv_sem=d_recv.at[6 - n],
            device_id=device(offset_of(code)),
            device_id_type=MESH,
        )
        for n, code in enumerate(MOVE_CODES)
        if code != 13
    ]
    for copy in d_copies:
        copy.start()

    for copy in b_copies:
        copy.wait()
    for side in range(2):
        at = PAD - 1 if side == 0 else PAD + CY
        for n, d in enumerate(Y_MOVERS[side]):
            tile = yr[side, n]
            if n == 1:
                tile = jnp.where(sub == 0, ye[side, 0], tile)
            if n == 2:
                tile = jnp.where(sub == CX - 1, ye[side, 1], tile)
            for x in range(CX):
                rel[PLACE[d], x + 1 - LATTICE[d][0], at : at + 1, :] = tile[x : x + 1, :]
    columns = []
    for side in range(2):
        tile = zr[side]
        tile = jnp.where((sub == 1) & (lane < CY), ze[side, 0], tile)
        tile = jnp.where((sub == 2) & (lane >= 128 - CY), ze[side, 1], tile)
        tile = jnp.where((sub == 3) & ((lane & 15) == 0), ze[side, 2], tile)
        tile = jnp.where((sub == 4) & ((lane & 15) == 15), ze[side, 3], tile)
        columns.append(tile)
    zm[...] = jnp.transpose(
        jnp.concatenate(columns + [jnp.zeros((112, 128), jnp.float32)], axis=0)
    )

    low_wall = [here[n] == 0 for n in range(3)]
    high_wall = [here[n] == sizes[n] - 1 for n in range(3)]

    def stream(x, carry):
        for half in range(2):
            rows = pl.ds(8 * half, 8)
            beside = zm[pl.ds(pl.multiple_of(CY * x + 8 * half, 8), 8), :]
            walls = {
                (0, 1): low_wall[0] & (x == 0),
                (0, -1): high_wall[0] & (x == CX - 1),
                (2, 1): low_wall[2] & (lane == 0),
                (2, -1): high_wall[2] & (lane == 127),
            }
            if half == 0:
                walls[(1, 1)] = low_wall[1] & (sub == 0)
            else:
                walls[(1, -1)] = high_wall[1] & (sub == 7)
            for d in range(19):
                vector = LATTICE[d]
                value = rel[
                    PLACE[d], x + 1 - vector[0], pl.ds(PAD + 8 * half - vector[1], 8), :
                ]
                if vector[2] != 0:
                    side = 0 if vector[2] == 1 else 1
                    column = 8 * side + Z_MOVERS[side].index(d)
                    edge = 0 if side == 0 else 127
                    value = jnp.where(
                        lane == edge,
                        beside[:, column : column + 1],
                        pltpu.roll(value, vector[2] % 128, 1),
                    )
                blocked = None
                for axis in range(3):
                    wall = walls.get((axis, vector[axis]))
                    if vector[axis] != 0 and wall is not None:
                        blocked = wall if blocked is None else blocked | wall
                if blocked is not None:
                    back = rel[PLACE[OPPOSITE[d]], x + 1, pl.ds(PAD + 8 * half, 8), :]
                    value = jnp.where(blocked, back, value)
                out_pop[d, x, rows, :] = value
        return carry

    lax.fori_loop(0, CX, stream, 0)

    for copy in d_copies:
        copy.wait()
    arrived = ds[3]
    for n in range(7):
        if n != 3:
            arrived = arrived + dr[n]
    out_part[0, 0, 0] = arrived[0:6, :]


def body(sizes, *args):
    f32, i32 = jnp.float32, jnp.int32
    vmem = pltpu.VMEM
    sems = pltpu.SemaphoreType.DMA
    return pl.pallas_call(
        lambda *refs: kernel(sizes, *refs),
        out_shape=(
            jax.ShapeDtypeStruct((19, CX, CY, CZ), f32),
            jax.ShapeDtypeStruct((1, 1, 1, 6, SLOTS), f32),
        ),
        in_specs=[pl.BlockSpec(memory_space=pl.ANY)] * 8,
        out_specs=(
            pl.BlockSpec(memory_space=vmem),
            pl.BlockSpec(memory_space=vmem),
        ),
        scratch_shapes=[
            vmem((19, CX, CY, CZ), f32),
            vmem((CX, CY, CZ), f32),
            vmem((CX, CY, CZ), i32),
            vmem((1, TOUCHES), i32),
            vmem((CANDIDATES, SLOTS), i32),
            vmem((1, SLOTS), i32),
            vmem((1, SLOTS), i32),
            vmem((27, 8, 128), f32),
            vmem((5, CX, CY, CZ), f32),
            vmem((8 * CX * CY, CZ), f32),
            vmem((14, 8, 128), i32),
            vmem((8, 8, 128), i32),
            vmem((28, 4, 128), f32),
            vmem((27, 4, 128), f32),
            vmem((19, CX + 2, CY + 2 * PAD, CZ), f32),
            vmem((2, 5, CX, CZ), f32),
            vmem((2, 5, CX, CZ), f32),
            vmem((2, 2, CX, CZ), f32),
            vmem((CX * CY, 128), f32),
            vmem((2, 8, 128), f32),
            vmem((2, 8, 128), f32),
            vmem((2, 4, 8, 128), f32),
            vmem((8, 128), f32),
            vmem((7, 8, 128), f32),
            vmem((7, 8, 128), f32),
            sems((7,)),
            sems((CX,)),
            sems((27,)),
            sems((27,)),
            sems((18,)),
            sems((18,)),
            sems((27,)),
            sems((27,)),
            sems((7,)),
            sems((7,)),
        ],
        compiler_params=pltpu.CompilerParams(collective_id=0, has_side_effects=True),
    )(*args)


def solution(mesh):
    sizes = tuple(mesh.shape[axis] for axis in AXES)
    cells, blocks = P(*AXES), P(*AXES, None)
    records = P(*AXES, None, None)
    fields = P(None, *AXES)
    return jax.shard_map(
        lambda *args: body(sizes, *args),
        mesh=mesh,
        in_specs=(fields, cells, cells, blocks, records, records, blocks, blocks),
        out_specs=(fields, records),
        check_vma=False,
    )
```

time: 243 us -> 34.1 us (0.14)
  the two profiles are of different devices: /device:TPU:105 before, /device:TPU:1 now
where the time goes in v1:
time: 34.1 us; the launch traced here: 33.8 us
  Pallas kernels  26.9 us (79%)
  local copies, waits for them, and re-layouts  6.26 us (18%)
  between operations  0.64 us (2%)
    pallas_call x1, Pallas kernels, body(): pl.pallas_call(lambda *refs: kernel(sizes, *refs), out_shape=(jax.ShapeDt...  26.9 us
    unnamed x3, local copies, waits for them, and re-layouts  5 us
    pallas_call x1, local copies, waits for them, and re-layouts, body(): pl.pallas_call(lambda *refs: kernel(sizes, *refs), out_shape=(jax.ShapeDt...  1.26 us

profile of v1, /device:TPU:1, one launch (start us, length us, event | category | flops | bytes accessed | tf_op | source)
XLA Modules:
  0.0 33.8 jit_solution(5333632648654556463)
XLA Ops:
  0.6 1.3 %copy.10.refs_4_ = f32[1,1,1,6,128]{4,3,2,1,0:T(8,128)} copy(f32[1,1,1,6,128]{4,2,3,1,0:T(1,128)} %param.12) | data formatting | bytes 6144 | tf_op args[4]
  1.9 1.3 %copy.11.refs_5_ = s32[1,1,1,12,128]{4,3,2,1,0:T(8,128)} copy(s32[1,1,1,12,128]{4,2,3,1,0:T(1,128)} %param.13) | data formatting | bytes 12288 | tf_op args[5]
  3.2 26.9 %shard_map.95 = (f32[19,8,16,128]{3,2,1,0:T(8,128)}, f32[1,1,1,6,128]{4,3,2,1,0:T(8,128)}) custom-call(f32[19,8,16,128]{3,2,1,0:T(8,128)} %refs_0_.1, f32[8,16,128]{2,1,0:T(8,128)} %refs_1_.1, s32[8,16,128]{2,1,0:T(8,128)} %refs_2_.1, s32[1,1,1,256]{3,2,1,0:T(1,128)} %refs_3_.1, f32[1,1,1,6,128]{4,3,2,1,0:T(8,128)} %copy.10.refs_4_, ...), custom_call_target="tpu_custom_call" | custom-call | tf_op jit(solution)/shard_map/pallas_call | solution.py:582
  30.1 1.3 %copy.12 = f32[1,1,1,6,128]{4,2,3,1,0:T(1,128)} copy(f32[1,1,1,6,128]{4,3,2,1,0:T(8,128)} %get-tuple-element.3) | data formatting | bytes 6144 | tf_op jit(solution)/shard_map/pallas_call | solution.py:582
  31.4 2.4 %copy.14 = f32[19,8,16,128]{3,2,1,0:T(8,128)} copy(f32[19,8,16,128]{3,2,1,0:T(8,128)} %get-tuple-element.6) | data formatting | bytes 2490368

commit v2 on v1

v2 whole, which is shorter than its diff:
```python
import jax
import jax.numpy as jnp
from jax import lax
from jax.experimental import pallas as pl
from jax.experimental.pallas import tpu as pltpu
from jax.sharding import PartitionSpec as P

LATTICE = [
    (0, 0, 0),
    (1, 0, 0),
    (-1, 0, 0),
    (0, 1, 0),
    (0, -1, 0),
    (0, 0, 1),
    (0, 0, -1),
    (1, 1, 0),
    (-1, -1, 0),
    (1, -1, 0),
    (-1, 1, 0),
    (1, 0, 1),
    (-1, 0, -1),
    (1, 0, -1),
    (-1, 0, 1),
    (0, 1, 1),
    (0, -1, -1),
    (0, 1, -1),
    (0, -1, 1),
]
OPPOSITE = [0, 2, 1, 4, 3, 6, 5, 8, 7, 10, 9, 12, 11, 14, 13, 16, 15, 18, 17]
WEIGHTS = [1.0 / 3.0] + [1.0 / 18.0] * 6 + [1.0 / 36.0] * 12
PAIRS = [(i, i + 1) for i in range(1, 19, 2)]
RELAX_TIME = 0.8
SPEED_UNIT = 0.05
FORCE_SCALE = 0.1
CONTACT_GAIN = 1.0
GRAVITY_STEP = 0.1
R = 8.0
CX, CY, CZ, SLOTS, TOUCHES, CANDIDATES = 8, 16, 128, 128, 256, 12
SPANS = (CX / R, CY / R, CZ / R)
AXES = ("gx", "gy", "gz")
MESH = pl.DeviceIdType.MESH

X_UP, X_DOWN = [1, 7, 9, 11, 13], [2, 8, 10, 12, 14]
Y_MOVERS = [[3, 7, 10, 15, 17], [4, 9, 8, 18, 16]]
Z_MOVERS = [[5, 11, 14, 15, 18], [6, 13, 12, 17, 16]]
PLACE = {d: n for n, d in enumerate(X_UP + X_DOWN + [0, 3, 4, 5, 6, 15, 16, 17, 18])}
MOVE_CODES = [4, 10, 12, 13, 14, 16, 22]
PAD = 8
STRIDE = CY + 2 * PAD


def offset_of(code):
    return (code // 9 - 1, code // 3 % 3 - 1, code % 3 - 1)


def projected(velocity, d):
    along = None
    for n in range(3):
        if LATTICE[d][n] == 1:
            along = velocity[n] if along is None else along + velocity[n]
        elif LATTICE[d][n] == -1:
            along = -velocity[n] if along is None else along - velocity[n]
    return along


def lane_gather(table, index):
    return jnp.take_along_axis(table, index, axis=1, mode="promise_in_bounds")


def dot_lanes(a, b):
    return lax.dot_general(a, b, (((1,), (1,)), ((), ())), preferred_element_type=jnp.float32)


def kernel(
    sizes,
    pop,
    frac,
    inter,
    touch,
    part,
    cont,
    dcode,
    dslot,
    rel_out,
    col_out,
    out_part,
    f_v,
    frac_v,
    int_v,
    touch_v,
    cont_v,
    dcode_v,
    dslot_v,
    nb,
    mac,
    split,
    inv_v,
    inv2_v,
    cs,
    cr,
    zc,
    xs,
    xr,
    ys,
    yr,
    ye,
    zm,
    zs,
    zr,
    ze,
    rec,
    ds,
    dr,
    in_sem,
    pop_sem,
    a_send,
    a_recv,
    b_send,
    b_recv,
    c_send,
    c_recv,
    d_send,
    d_recv,
):
    rel = rel_out
    here = [lax.axis_index(axis) for axis in AXES]

    def device(offset):
        return tuple(
            here[n] if offset[n] == 0 else lax.rem(here[n] + offset[n] + sizes[n], sizes[n])
            for n in range(3)
        )

    def exists(offset):
        ok = None
        for n in range(3):
            if offset[n] != 0:
                test = here[n] > 0 if offset[n] < 0 else here[n] < sizes[n] - 1
                ok = test if ok is None else ok & test
        return ok

    others = [code for code in range(27) if code != 13]
    others.sort(key=lambda code: -sum(abs(step) for step in offset_of(code)))
    ok = {code: exists(offset_of(code)) for code in others}
    around = [
        1 + (here[n] > 0).astype(jnp.int32) + (here[n] < sizes[n] - 1).astype(jnp.int32)
        for n in range(3)
    ]

    def start_all(make):
        for code in others:
            pl.when(ok[code])(lambda code=code: make(code).start())

    def wait_all(make):
        for code in others:

            @pl.when(ok[code])
            def _(code=code):
                make(26 - code).wait_recv()
                make(code).wait_send()

    barrier = pltpu.get_barrier_semaphore()
    for code in others:

        @pl.when(ok[code])
        def _(code=code):
            pl.semaphore_signal(
                barrier, inc=1, device_id=device(offset_of(code)), device_id_type=MESH
            )

    small = [
        (part.at[0, 0, :, 0], nb.at[13, pl.ds(0, 6)]),
        (touch.at[0, 0], touch_v),
        (dcode.at[0, 0], dcode_v),
        (dslot.at[0, 0], dslot_v),
        (frac, frac_v),
        (inter, int_v),
        (cont.at[0, 0, :, 0], cont_v),
    ]
    loads = [pltpu.make_async_copy(s, d, in_sem.at[n]) for n, (s, d) in enumerate(small)]
    for load in loads:
        load.start()

    def pop_load(x):
        return pltpu.make_async_copy(
            pop.at[:, pl.ds(CY * x, CY)], f_v.at[:, pl.ds(CY * x, CY)], pop_sem.at[x]
        )

    for x in range(CX):
        pop_load(x).start()

    lane = lax.broadcasted_iota(jnp.int32, (8, 128), 1)
    sub = lax.broadcasted_iota(jnp.int32, (8, 128), 0)

    loads[0].wait()
    pl.semaphore_wait(barrier, around[0] * around[1] * around[2] - 1)

    def send_a(code):
        return pltpu.make_async_remote_copy(
            src_ref=nb.at[13],
            dst_ref=nb.at[26 - code],
            send_sem=a_send.at[code],
            recv_sem=a_recv.at[26 - code],
            device_id=device(offset_of(code)),
            device_id_type=MESH,
        )

    start_all(send_a)

    loads[1].wait()
    loads[2].wait()
    loads[3].wait()
    entry = touch_v[0:1, :]
    wide = lax.broadcasted_iota(jnp.int32, (112, TOUCHES), 1)
    row = lax.broadcasted_iota(jnp.int32, (112, TOUCHES), 0)
    named = jnp.where((entry >> 7) == (row >> 2), wide + 1, 0).astype(jnp.float32)
    slot_row = lax.broadcasted_iota(jnp.int32, (SLOTS, TOUCHES), 0)
    placed = jnp.where((entry & 127) == slot_row, 1.0, 0.0)
    inverse = dot_lanes(named.astype(jnp.bfloat16), placed.astype(jnp.bfloat16))
    inv_v[...] = (inverse.astype(jnp.int32) - 1).reshape(14, 8, 128)
    code_row = jnp.broadcast_to(dcode_v[0:1, :], (8, 128))
    moved = jnp.concatenate(
        [jnp.where(code_row == code, lane + 1, 0).astype(jnp.float32) for code in MOVE_CODES]
        + [jnp.zeros((8, 128), jnp.float32)],
        axis=0,
    )
    tall = lax.broadcasted_iota(jnp.int32, (SLOTS, SLOTS), 0)
    landing = jnp.where(dslot_v[0:1, :] == tall, 1.0, 0.0)
    inverse2 = dot_lanes(moved.astype(jnp.bfloat16), landing.astype(jnp.bfloat16))
    inv2_v[...] = (inverse2.astype(jnp.int32) - 1).reshape(8, 8, 128)

    loads[4].wait()
    loads[5].wait()

    def moments(x, carry):
        pop_load(x).wait()
        for half in range(2):
            start = pl.multiple_of(CY * x + 8 * half, 8)
            rows = pl.ds(start, 8)
            f = [f_v[d, rows, :] for d in range(19)]
            rho = f[0]
            momentum = [None, None, None]
            for d in range(1, 19):
                rho = rho + f[d]
            for n in range(3):
                for d in range(1, 19):
                    if LATTICE[d][n] == 1:
                        momentum[n] = f[d] if momentum[n] is None else momentum[n] + f[d]
                for d in range(1, 19):
                    if LATTICE[d][n] == -1:
                        momentum[n] = momentum[n] - f[d]
            eps = frac_v[rows, :]
            weight = jnp.where(
                int_v[rows, :] < TOUCHES,
                eps * (RELAX_TIME - 0.5) / (1.0 - eps + (RELAX_TIME - 0.5)),
                0.0,
            )
            scale = 1.0 / rho
            mac[0, rows, :] = rho
            mac[1, rows, :] = weight
            for n in range(3):
                mac[2 + n, rows, :] = momentum[n] * scale
            for n, term in enumerate(momentum + [rho]):
                term = term * weight
                if n == 3:
                    mac[5, rows, :] = term
                high = term.astype(jnp.bfloat16).astype(jnp.float32)
                split[pl.ds(8 * start + n, 8, stride=8), :] = high
                split[pl.ds(8 * start + 4 + n, 8, stride=8), :] = term - high
        return carry

    lax.fori_loop(0, CX, moments, 0, unroll=2)

    low_row = lax.broadcasted_iota(jnp.int32, (32, 128), 0)

    def add_slab(x, total):
        left, right = [], []
        for y in range(CY):
            slots = int_v[pl.ds(CY * x + y, 1), :]
            tile = split[pl.ds(pl.multiple_of(8 * (CY * x + y), 8), 8), :]
            upper = jnp.broadcast_to(slots >> 5, (8, 128))
            picked = [jnp.where(upper == a, tile, 0.0) for a in range(8)]
            left.append(jnp.concatenate(picked, axis=0).astype(jnp.bfloat16))
            lower = jnp.broadcast_to(slots & 31, (32, 128))
            right.append(jnp.where(lower == low_row, 1.0, 0.0).astype(jnp.bfloat16))
        return total + dot_lanes(
            jnp.concatenate(left, axis=1), jnp.concatenate(right, axis=1)
        )

    total = lax.fori_loop(0, CX, add_slab, jnp.zeros((64, 32), jnp.float32), unroll=4)
    tables = []
    for h in range(2):
        table = jnp.concatenate(
            [total[8 * a : 8 * a + 8, :] for a in range(4 * h, 4 * h + 4)], axis=1
        )
        tables.append(table + pltpu.roll(table, 4, 0))

    for q in range(14):
        source = inv_v[q]
        index = source & 127
        picked = jnp.where(
            source < 128, lane_gather(tables[0], index), lane_gather(tables[1], index)
        )
        picked = jnp.where(source >= 0, picked, 0.0)
        cs[2 * q] = picked[0:4, :]
        cs[2 * q + 1] = picked[4:8, :]

    def send_c(code):
        return pltpu.make_async_remote_copy(
            src_ref=cs.at[code],
            dst_ref=cr.at[26 - code],
            send_sem=c_send.at[code],
            recv_sem=c_recv.at[26 - code],
            device_id=device(offset_of(code)),
            device_id_type=MESH,
        )

    start_all(send_c)

    def cell_rows(x, half):
        cells = pl.ds(pl.multiple_of(CY * x + 8 * half, 8), 8)
        return cells, pl.ds(pl.multiple_of(STRIDE * (x + 1) + PAD + 8 * half, 8), 8)

    def relax(x, carry):
        for half in range(2):
            rows, dest = cell_rows(x, half)
            rho = mac[0, rows, :]
            weight = mac[1, rows, :]
            u = [mac[2 + n, rows, :] for n in range(3)]
            alpha = (1.0 - weight) * (1.0 / RELAX_TIME)
            keep = 1.0 - alpha - weight
            even = (alpha - weight) * rho
            odd = 3.0 * (alpha + weight) * rho
            base = even * (1.0 - 1.5 * (u[0] * u[0] + u[1] * u[1] + u[2] * u[2]))
            even = 4.5 * even
            rel[PLACE[0], dest, :] = (1.0 - alpha) * f_v[0, rows, :] + WEIGHTS[0] * base
            for i, j in PAIRS:
                along = projected(u, i)
                symmetric = WEIGHTS[i] * (base + even * along * along)
                skew = WEIGHTS[i] * (odd * along)
                fi, fj = f_v[i, rows, :], f_v[j, rows, :]
                rel[PLACE[i], dest, :] = keep * fi + weight * fj + (symmetric + skew)
                rel[PLACE[j], dest, :] = keep * fj + weight * fi + (symmetric - skew)
        return carry

    lax.fori_loop(0, CX, relax, 0, unroll=2)

    def pack_ends(x, carry):
        for half in range(2):
            rows, dest = cell_rows(x, half)
            packed = jnp.zeros((8, 128), jnp.float32)
            for side in range(2):
                edge = 127 if side == 0 else 0
                values = [rel[PLACE[d], dest, :] for d in Z_MOVERS[side]]
                values += [mac[5, rows, :], int_v[rows, :].astype(jnp.float32)]
                for n, value in enumerate(values):
                    packed = jnp.where(lane == 8 * side + n, value[:, edge : edge + 1], packed)
            zm[rows, :] = packed
        return carry

    lax.fori_loop(0, CX, pack_ends, 0, unroll=CX)
    zc[...] = jnp.transpose(zm[...])[0:16, :]

    wait_all(send_a)

    for code in others:
        nb[code] = jnp.where(ok[code], nb[code], 0.0)

    touch_code = [jnp.broadcast_to(touch_v[0:1, pl.ds(128 * h, 128)] >> 7, (8, 128)) for h in range(2)]
    touch_slot = [jnp.broadcast_to(touch_v[0:1, pl.ds(128 * h, 128)] & 127, (8, 128)) for h in range(2)]

    def find_velocity(code, found):
        tile = nb[code]
        return tuple(
            jnp.where(touch_code[h] == code, lane_gather(tile, touch_slot[h]), found[h])
            for h in range(2)
        )

    zero = jnp.zeros((8, 128), jnp.float32)
    found = lax.fori_loop(0, 27, find_velocity, (zero, zero), unroll=27)
    speed = [
        [jnp.broadcast_to(SPEED_UNIT * found[h][3 + n : 4 + n, :], (8, 128)) for n in range(3)]
        for h in range(2)
    ]

    def solid_part(slots, mass):
        index = slots & 127
        first = slots < 128
        v = [
            jnp.where(first, lane_gather(speed[0][n], index), lane_gather(speed[1][n], index))
            for n in range(3)
        ]
        base = mass * (1.0 - 1.5 * (v[0] * v[0] + v[1] * v[1] + v[2] * v[2]))
        return v, base, 4.5 * mass, 3.0 * mass

    def solid_term(parts, d):
        v, base, even, odd = parts
        along = projected(v, d)
        return WEIGHTS[d] * (base + along * (even * along + odd))

    for side in range(2):
        x = CX - 1 if side == 0 else 0
        for half in range(2):
            rows, dest = cell_rows(x, half)
            parts = solid_part(int_v[rows, :], mac[5, rows, :])
            for n, d in enumerate((X_UP, X_DOWN)[side]):
                value = rel[PLACE[d], dest, :] + solid_term(parts, d)
                xs[side, n, pl.ds(8 * half, 8), :] = value
    for side in range(2):
        y = CY - 1 if side == 0 else 0
        rows = pl.ds(y, CX, stride=CY)
        dest = pl.ds(STRIDE + PAD + y, CX, stride=STRIDE)
        parts = solid_part(int_v[rows, :], mac[5, rows, :])
        for n, d in enumerate(Y_MOVERS[side]):
            value = rel[PLACE[d], dest, :] + solid_term(parts, d)
            if LATTICE[d][0] != 0:
                value = pltpu.roll(value, LATTICE[d][0] % CX, 0)
            ys[side, n] = value
    for side in range(2):
        slots = jnp.broadcast_to(zc[8 * side + 6 : 8 * side + 7, :].astype(jnp.int32), (8, 128))
        mass = jnp.broadcast_to(zc[8 * side + 5 : 8 * side + 6, :], (8, 128))
        v, base, even, odd = solid_part(slots, mass)
        along = zero
        share = jnp.full((8, 128), 1.0 / 36.0, jnp.float32)
        for n, d in enumerate(Z_MOVERS[side]):
            along = jnp.where(sub == n, projected(v, d), along)
        share = jnp.where(sub == 0, 1.0 / 18.0, share)
        tile = zc[8 * side : 8 * side + 8, :] + share * (base + along * (even * along + odd))
        up_y = jnp.where((lane & 15) == 0, pltpu.roll(tile, 128 - 15, 1), pltpu.roll(tile, 1, 1))
        down_y = jnp.where((lane & 15) == 15, pltpu.roll(tile, 15, 1), pltpu.roll(tile, 127, 1))
        moved_z = jnp.where(sub == 1, pltpu.roll(tile, 16, 1), tile)
        moved_z = jnp.where(sub == 2, pltpu.roll(tile, 112, 1), moved_z)
        moved_z = jnp.where(sub == 3, up_y, moved_z)
        zs[side] = jnp.where(sub == 4, down_y, moved_z)

    moves = []
    for side in range(2):
        step = 1 - 2 * side
        moves.append((xs.at[side], xr.at[side], (step, 0, 0)))
        moves.append((ys.at[side], yr.at[side], (0, step, 0)))
        moves.append((ys.at[side, 1], ye.at[side, 0], (1, step, 0)))
        moves.append((ys.at[side, 2], ye.at[side, 1], (-1, step, 0)))
        moves.append((zs.at[side], zr.at[side], (0, 0, step)))
        moves.append((zs.at[side], ze.at[side, 0], (1, 0, step)))
        moves.append((zs.at[side], ze.at[side, 1], (-1, 0, step)))
        moves.append((zs.at[side], ze.at[side, 2], (0, 1, step)))
        moves.append((zs.at[side], ze.at[side, 3], (0, -1, step)))
    def send_b(n):
        source, target, offset = moves[n]
        return pltpu.make_async_remote_copy(
            src_ref=source,
            dst_ref=target,
            send_sem=b_send.at[n],
            recv_sem=b_recv.at[n],
            device_id=device(offset),
            device_id_type=MESH,
        )

    def code_of(offset):
        return 9 * (offset[0] + 1) + 3 * (offset[1] + 1) + offset[2] + 1

    for n in range(len(moves)):
        pl.when(ok[code_of(moves[n][2])])(lambda n=n: send_b(n).start())

    def solid(x, carry):
        for half in range(2):
            rows, dest = cell_rows(x, half)
            v, base, even, odd = solid_part(int_v[rows, :], mac[5, rows, :])
            rel[PLACE[0], dest, :] = rel[PLACE[0], dest, :] + WEIGHTS[0] * base
            for i, j in PAIRS:
                along = projected(v, i)
                symmetric = WEIGHTS[i] * (base + even * along * along)
                skew = WEIGHTS[i] * (odd * along)
                rel[PLACE[i], dest, :] = rel[PLACE[i], dest, :] + (symmetric + skew)
                rel[PLACE[j], dest, :] = rel[PLACE[j], dest, :] + (symmetric - skew)
        return carry

    lax.fori_loop(0, CX, solid, 0, unroll=CX)

    loads[6].wait()
    listed = [
        cont_v[0:8, :],
        jnp.concatenate([cont_v[8:12, :], jnp.full((4, 128), 27 * SLOTS, jnp.int32)], axis=0),
    ]
    listed_code = [entries >> 7 for entries in listed]
    listed_slot = [entries & 127 for entries in listed]

    def find_partner(code, partner):
        shifts = (code // 9 - 1, code // 3 % 3 - 1, code % 3 - 1)
        result = []
        for n in range(3):
            line = nb[code, pl.ds(n, 1), :] + shifts[n].astype(jnp.float32) * SPANS[n]
            line = jnp.broadcast_to(line, (8, 128))
            for h in range(2):
                result.append(
                    jnp.where(
                        listed_code[h] == code,
                        lane_gather(line, listed_slot[h]),
                        partner[2 * n + h],
                    )
                )
        return tuple(result)

    partner = lax.fori_loop(0, 27, find_partner, (zero,) * 6, unroll=27)
    force = [None, None, None]
    for h in range(2):
        apart = [nb[13, n : n + 1, :] - partner[2 * n + h] for n in range(3)]
        square = apart[0] * apart[0] + apart[1] * apart[1] + apart[2] * apart[2]
        soften = 1.0 + 0.25 * square
        strength = jnp.where(listed_code[h] < 27, CONTACT_GAIN / (soften * soften), 0.0)
        for n in range(3):
            term = jnp.sum(apart[n] * strength, axis=0, keepdims=True)
            force[n] = term if h == 0 else force[n] + term

    wait_all(send_c)
    hydro = cs[13]
    for code in others:
        hydro = hydro + jnp.where(ok[code], cr[code], 0.0)
    rec[6:8, :] = jnp.zeros((2, 128), jnp.float32)
    for n in range(3):
        speed_old = nb[13, 3 + n : 4 + n, :]
        pulled = hydro[n : n + 1, :] - (SPEED_UNIT * speed_old) * hydro[3:4, :]
        speed_new = speed_old + FORCE_SCALE * pulled + force[n]
        if n == 2:
            speed_new = speed_new - GRAVITY_STEP
        rec[3 + n : 4 + n, :] = speed_new
        rec[n : n + 1, :] = nb[13, n : n + 1, :] + speed_new * (SPEED_UNIT / R)

    record = rec[...]
    for n, code in enumerate(MOVE_CODES):
        shift = zero
        for axis, step in enumerate(offset_of(code)):
            if step != 0:
                shift = jnp.where(sub == axis, step * SPANS[axis], shift)
        source = inv2_v[n]
        picked = lane_gather(record - shift, source & 127)
        ds[n] = jnp.where(source >= 0, picked, 0.0)
    def send_d(n):
        return pltpu.make_async_remote_copy(
            src_ref=ds.at[n],
            dst_ref=dr.at[6 - n],
            send_sem=d_send.at[n],
            recv_sem=d_recv.at[6 - n],
            device_id=device(offset_of(MOVE_CODES[n])),
            device_id_type=MESH,
        )

    movers = [n for n in range(7) if MOVE_CODES[n] != 13]
    for n in movers:
        pl.when(ok[MOVE_CODES[n]])(lambda n=n: send_d(n).start())

    for n in movers:

        @pl.when(ok[MOVE_CODES[n]])
        def _(n=n):
            send_d(6 - n).wait_recv()
            send_d(n).wait_send()

    arrived = ds[3]
    for n in movers:
        arrived = arrived + jnp.where(ok[MOVE_CODES[n]], dr[n], 0.0)
    out_part[0, 0, :, 0, :] = arrived[0:6, :]

    for n in range(len(moves)):
        there = moves[n][2]

        @pl.when(ok[26 - code_of(there)])
        def _(n=n):
            send_b(n).wait_recv()

        @pl.when(ok[code_of(there)])
        def _(n=n):
            send_b(n).wait_send()

    for side in range(2):
        x = -1 if side == 0 else CX
        for n, d in enumerate((X_UP, X_DOWN)[side]):
            rel[PLACE[d], pl.ds(STRIDE * (x + 1) + PAD, CY), :] = xr[side, n]
    for side in range(2):
        y = -1 if side == 0 else CY
        for n, d in enumerate(Y_MOVERS[side]):
            tile = yr[side, n]
            if n == 1:
                tile = jnp.where(sub == 0, ye[side, 0], tile)
            if n == 2:
                tile = jnp.where(sub == CX - 1, ye[side, 1], tile)
            start = STRIDE * (1 - LATTICE[d][0]) + PAD + y
            rel[PLACE[d], pl.ds(start, CX, stride=STRIDE), :] = tile
    columns = []
    for side in range(2):
        tile = zr[side]
        tile = jnp.where((sub == 1) & (lane < CY), ze[side, 0], tile)
        tile = jnp.where((sub == 2) & (lane >= 128 - CY), ze[side, 1], tile)
        tile = jnp.where((sub == 3) & ((lane & 15) == 0), ze[side, 2], tile)
        tile = jnp.where((sub == 4) & ((lane & 15) == 15), ze[side, 3], tile)
        columns.append(tile)
    col_out[...] = jnp.transpose(
        jnp.concatenate(columns + [jnp.zeros((112, 128), jnp.float32)], axis=0)
    )


def stream_kernel(sizes, rel, columns, records, out_pop, out_part, out_v, out_sem, part_sem):
    here = [lax.axis_index(axis) for axis in AXES]
    keep_records = pltpu.make_async_copy(records, out_part, part_sem.at[0])
    keep_records.start()
    lane = lax.broadcasted_iota(jnp.int32, (8, 128), 1)
    sub = lax.broadcasted_iota(jnp.int32, (8, 128), 0)
    low_wall = [here[n] == 0 for n in range(3)]
    high_wall = [here[n] == sizes[n] - 1 for n in range(3)]
    order = sorted(range(19), key=lambda d: LATTICE[d][2] != 0)

    def put(d):
        return pltpu.make_async_copy(out_v.at[d], out_pop.at[d], out_sem.at[d])

    for d in order:
        vector = LATTICE[d]
        for x in range(CX):
            for half in range(2):
                cells = pl.ds(CY * x + 8 * half, 8)
                walls = {
                    (0, 1): low_wall[0] if x == 0 else None,
                    (0, -1): high_wall[0] if x == CX - 1 else None,
                    (1, 1): low_wall[1] & (sub == 0) if half == 0 else None,
                    (1, -1): high_wall[1] & (sub == 7) if half == 1 else None,
                    (2, 1): low_wall[2] & (lane == 0),
                    (2, -1): high_wall[2] & (lane == 127),
                }
                start = STRIDE * (x + 1 - vector[0]) + PAD + 8 * half - vector[1]
                value = rel[PLACE[d], pl.ds(start, 8), :]
                if vector[2] != 0:
                    side = 0 if vector[2] == 1 else 1
                    column = 8 * side + Z_MOVERS[side].index(d)
                    value = jnp.where(
                        lane == (0 if side == 0 else 127),
                        columns[cells, column : column + 1],
                        pltpu.roll(value, vector[2] % 128, 1),
                    )
                blocked = None
                for axis in range(3):
                    wall = walls.get((axis, vector[axis]))
                    if wall is not None:
                        blocked = wall if blocked is None else blocked | wall
                if blocked is not None:
                    back = rel[PLACE[OPPOSITE[d]], pl.ds(STRIDE * (x + 1) + PAD + 8 * half, 8), :]
                    value = jnp.where(blocked, back, value)
                out_v[d, cells, :] = value
        put(d).start()
    for d in order:
        put(d).wait()
    keep_records.wait()


def body(sizes, pop, frac, inter, touch, part, cont, dcode, dslot):
    f32, i32 = jnp.float32, jnp.int32
    cells = CX * CY
    part, cont = (jnp.transpose(a, (0, 1, 3, 2, 4)) for a in (part, cont))
    args = (
        pop.reshape(19, cells, CZ),
        frac.reshape(cells, CZ),
        inter.reshape(cells, CZ),
        touch,
        part,
        cont,
        dcode,
        dslot,
    )
    vmem = pltpu.VMEM
    sems = pltpu.SemaphoreType.DMA
    in_vmem = pl.BlockSpec(memory_space=vmem)
    in_any = pl.BlockSpec(memory_space=pl.ANY)
    relaxed, columns, records = pl.pallas_call(
        lambda *refs: kernel(sizes, *refs),
        out_shape=(
            vmem((19, STRIDE * (CX + 2), CZ), f32),
            vmem((cells, 128), f32),
            vmem((1, 1, 6, 1, SLOTS), f32),
        ),
        in_specs=[in_any] * 8,
        out_specs=(in_vmem,) * 3,
        scratch_shapes=[
            vmem((19, cells, CZ), f32),
            vmem((cells, CZ), f32),
            vmem((cells, CZ), i32),
            vmem((1, TOUCHES), i32),
            vmem((CANDIDATES, SLOTS), i32),
            vmem((1, SLOTS), i32),
            vmem((1, SLOTS), i32),
            vmem((27, 8, 128), f32),
            vmem((6, cells, CZ), f32),
            vmem((8 * cells, CZ), f32),
            vmem((14, 8, 128), i32),
            vmem((8, 8, 128), i32),
            vmem((28, 4, 128), f32),
            vmem((27, 4, 128), f32),
            vmem((16, 128), f32),
            vmem((2, 5, CY, CZ), f32),
            vmem((2, 5, CY, CZ), f32),
            vmem((2, 5, CX, CZ), f32),
            vmem((2, 5, CX, CZ), f32),
            vmem((2, 2, CX, CZ), f32),
            vmem((cells, 128), f32),
            vmem((2, 8, 128), f32),
            vmem((2, 8, 128), f32),
            vmem((2, 4, 8, 128), f32),
            vmem((8, 128), f32),
            vmem((7, 8, 128), f32),
            vmem((7, 8, 128), f32),
            sems((7,)),
            sems((CX,)),
            sems((27,)),
            sems((27,)),
            sems((18,)),
            sems((18,)),
            sems((27,)),
            sems((27,)),
            sems((7,)),
            sems((7,)),
        ],
        compiler_params=pltpu.CompilerParams(collective_id=0, has_side_effects=True),
    )(*args)
    populations, records = pl.pallas_call(
        lambda *refs: stream_kernel(sizes, *refs),
        out_shape=(
            jax.ShapeDtypeStruct((19, cells, CZ), f32),
            jax.ShapeDtypeStruct((1, 1, 6, 1, SLOTS), f32),
        ),
        in_specs=[in_vmem] * 3,
        out_specs=(in_any,) * 2,
        scratch_shapes=[vmem((19, cells, CZ), f32), sems((19,)), sems((1,))],
    )(*(pltpu.with_memory_space_constraint(a, vmem) for a in (relaxed, columns, records)))
    return populations.reshape(19, CX, CY, CZ), jnp.transpose(records, (0, 1, 3, 2, 4))


def solution(mesh):
    sizes = tuple(mesh.shape[axis] for axis in AXES)
    cells, blocks = P(*AXES), P(*AXES, None)
    records = P(*AXES, None, None)
    fields = P(None, *AXES)
    return jax.shard_map(
        lambda *args: body(sizes, *args),
        mesh=mesh,
        in_specs=(fields, cells, cells, blocks, records, records, blocks, blocks),
        out_specs=(fields, records),
        check_vma=False,
    )
```

time: 34.1 us -> 20.4 us (0.60)
  Pallas kernels: 26.9 us -> 19.6 us
  local copies, waits for them, and re-layouts: 6.26 us -> 0 us
    pallas_call x1 -> x2, Pallas kernels: 26.9 us -> 19.6 us  [the longest x1 18.4 us: body(): pl.pallas_call(lambda *refs: kernel(sizes, *refs), out_shape=(vmem((19, S...]
    unnamed x3 -> x0, local copies, waits for them, and re-layouts: 5 us -> none
    pallas_call x1 -> x0, local copies, waits for them, and re-layouts: 1.26 us -> none  [body(): pl.pallas_call(lambda *refs: kernel(sizes, *refs), out_shape=(jax.ShapeDt...]
where the time goes in v2:
time: 20.4 us; the launch traced here: 20.2 us
  Pallas kernels  19.6 us (96%)
  between operations  0.64 us (3%)
    pallas_call x1, Pallas kernels, body(): pl.pallas_call(lambda *refs: kernel(sizes, *refs), out_shape=(vmem((19, S...  18.4 us
    pallas_call x1, Pallas kernels, body(): pl.pallas_call(lambda *refs: stream_kernel(sizes, *refs), out_shape=(jax....  1.24 us

profile of v2, /device:TPU:1, one launch (start us, length us, event | category | flops | bytes accessed | tf_op | source)
XLA Modules:
  0.0 20.2 jit_solution(18392096052135371084)
XLA Ops:
  0.6 18.4 %shard_map.95 = (f32[19,320,128]{2,1,0:T(8,128)S(1)}, f32[128,128]{1,0:T(8,128)S(1)}, f32[1,1,6,1,128]{4,3,2,1,0:T(1,128)S(1)}) custom-call(f32[19,128,128]{2,1,0:T(8,128)} %bitcast.9, f32[128,128]{1,0:T(8,128)} %bitcast.10, s32[128,128]{1,0:T(8,128)} %bitcast.11, s32[1,1,1,256]{3,2,1,0:T(1,128)} %refs_3_.1, f32[1,1,6,1,128]{4,3,2,1,0:T(1,128)} %bitcast.13, ...), custom_call_target="tpu_custom_call" | custom-call | tf_op jit(solution)/shard_map/pallas_call | solution.py:671
  19.0 1.2 %shard_map.96 = (f32[19,128,128]{2,1,0:T(8,128)}, f32[1,1,6,1,128]{4,3,2,1,0:T(1,128)}) custom-call(f32[19,320,128]{2,1,0:T(8,128)S(1)} %get-tuple-element.7.refs_0_, f32[128,128]{1,0:T(8,128)S(1)} %get-tuple-element.8.refs_1_, f32[1,1,6,1,128]{4,3,2,1,0:T(1,128)S(1)} %get-tuple-element.9.refs_2_), custom_call_target="tpu_custom_call" | custom-call | tf_op jit(solution)/shard_map/pallas_call | solution.py:721

commit v3 on v2

--- a/solution.py
+++ b/solution.py
@@ -112,7 +112,6 @@
     ds,
     dr,
     in_sem,
-    pop_sem,
     a_send,
     a_recv,
     b_send,
@@ -142,22 +141,30 @@
     others = [code for code in range(27) if code != 13]
     others.sort(key=lambda code: -sum(abs(step) for step in offset_of(code)))
     ok = {code: exists(offset_of(code)) for code in others}
-    around = [
-        1 + (here[n] > 0).astype(jnp.int32) + (here[n] < sizes[n] - 1).astype(jnp.int32)
-        for n in range(3)
-    ]
-
     def start_all(make):
         for code in others:
             pl.when(ok[code])(lambda code=code: make(code).start())
 
-    def wait_all(make):
-        for code in others:
-
-            @pl.when(ok[code])
-            def _(code=code):
-                make(26 - code).wait_recv()
-                make(code).wait_send()
+    count = [
+        (here[n] > 0).astype(jnp.int32) + (here[n] < sizes[n] - 1).astype(jnp.int32)
+        for n in range(3)
+    ]
+
+    neighbours = (count[0] + 1) * (count[1] + 1) * (count[2] + 1) - 1
+
+    def wait_rows(sem, rows):
+        pltpu.make_async_copy(split.at[pl.ds(0, rows)], split.at[pl.ds(0, rows)], sem).wait()
+
+    def wait_all(sem, rows):
+        for n in sorted({a * b * c - 1 for a in (2, 3) for b in (2, 3) for c in (2, 3)}):
+            pl.when(neighbours == n)(lambda n=n: wait_rows(sem, rows * n))
+
+    def wait_sides(sem, rows_of):
+        for a in (1, 2):
+            for b in (1, 2):
+                for c in (1, 2):
+                    here_now = (count[0] == a) & (count[1] == b) & (count[2] == c)
+                    pl.when(here_now)(lambda a=a, b=b, c=c: wait_rows(sem, rows_of(a, b, c)))
 
     barrier = pltpu.get_barrier_semaphore()
     for code in others:
@@ -168,152 +175,154 @@
                 barrier, inc=1, device_id=device(offset_of(code)), device_id_type=MESH
             )
 
-    small = [
-        (part.at[0, 0, :, 0], nb.at[13, pl.ds(0, 6)]),
+    own_load = pltpu.make_async_copy(part.at[0, 0, :, 0], nb.at[13, pl.ds(0, 6)], in_sem.at[0])
+    own_load.start()
+    for source, target in (
         (touch.at[0, 0], touch_v),
         (dcode.at[0, 0], dcode_v),
         (dslot.at[0, 0], dslot_v),
-        (frac, frac_v),
-        (inter, int_v),
         (cont.at[0, 0, :, 0], cont_v),
-    ]
-    loads = [pltpu.make_async_copy(s, d, in_sem.at[n]) for n, (s, d) in enumerate(small)]
-    for load in loads:
-        load.start()
+    ):
+        pltpu.make_async_copy(source, target, in_sem.at[1]).start()
+    for source, target in ((frac, frac_v), (inter, int_v)):
+        pltpu.make_async_copy(source, target, in_sem.at[2]).start()
 
     def pop_load(x):
         return pltpu.make_async_copy(
-            pop.at[:, pl.ds(CY * x, CY)], f_v.at[:, pl.ds(CY * x, CY)], pop_sem.at[x]
+            pop.at[:, pl.ds(64 * x, 64)], f_v.at[:, pl.ds(64 * x, 64)], in_sem.at[3 + x]
         )
 
-    for x in range(CX):
+    for x in range(2):
         pop_load(x).start()
 
     lane = lax.broadcasted_iota(jnp.int32, (8, 128), 1)
     sub = lax.broadcasted_iota(jnp.int32, (8, 128), 0)
-
-    loads[0].wait()
-    pl.semaphore_wait(barrier, around[0] * around[1] * around[2] - 1)
 
     def send_a(code):
         return pltpu.make_async_remote_copy(
             src_ref=nb.at[13],
             dst_ref=nb.at[26 - code],
-            send_sem=a_send.at[code],
-            recv_sem=a_recv.at[26 - code],
+            send_sem=a_send,
+            recv_sem=a_recv,
             device_id=device(offset_of(code)),
             device_id_type=MESH,
         )
-
-    start_all(send_a)
-
-    loads[1].wait()
-    loads[2].wait()
-    loads[3].wait()
-    entry = touch_v[0:1, :]
-    wide = lax.broadcasted_iota(jnp.int32, (112, TOUCHES), 1)
-    row = lax.broadcasted_iota(jnp.int32, (112, TOUCHES), 0)
-    named = jnp.where((entry >> 7) == (row >> 2), wide + 1, 0).astype(jnp.float32)
-    slot_row = lax.broadcasted_iota(jnp.int32, (SLOTS, TOUCHES), 0)
-    placed = jnp.where((entry & 127) == slot_row, 1.0, 0.0)
-    inverse = dot_lanes(named.astype(jnp.bfloat16), placed.astype(jnp.bfloat16))
-    inv_v[...] = (inverse.astype(jnp.int32) - 1).reshape(14, 8, 128)
-    code_row = jnp.broadcast_to(dcode_v[0:1, :], (8, 128))
-    moved = jnp.concatenate(
-        [jnp.where(code_row == code, lane + 1, 0).astype(jnp.float32) for code in MOVE_CODES]
-        + [jnp.zeros((8, 128), jnp.float32)],
-        axis=0,
-    )
-    tall = lax.broadcasted_iota(jnp.int32, (SLOTS, SLOTS), 0)
-    landing = jnp.where(dslot_v[0:1, :] == tall, 1.0, 0.0)
-    inverse2 = dot_lanes(moved.astype(jnp.bfloat16), landing.astype(jnp.bfloat16))
-    inv2_v[...] = (inverse2.astype(jnp.int32) - 1).reshape(8, 8, 128)
-
-    loads[4].wait()
-    loads[5].wait()
-
-    def moments(x, carry):
-        pop_load(x).wait()
-        for half in range(2):
-            start = pl.multiple_of(CY * x + 8 * half, 8)
-            rows = pl.ds(start, 8)
-            f = [f_v[d, rows, :] for d in range(19)]
-            rho = f[0]
-            momentum = [None, None, None]
-            for d in range(1, 19):
-                rho = rho + f[d]
-            for n in range(3):
-                for d in range(1, 19):
-                    if LATTICE[d][n] == 1:
-                        momentum[n] = f[d] if momentum[n] is None else momentum[n] + f[d]
-                for d in range(1, 19):
-                    if LATTICE[d][n] == -1:
-                        momentum[n] = momentum[n] - f[d]
-            eps = frac_v[rows, :]
-            weight = jnp.where(
-                int_v[rows, :] < TOUCHES,
-                eps * (RELAX_TIME - 0.5) / (1.0 - eps + (RELAX_TIME - 0.5)),
-                0.0,
-            )
-            scale = 1.0 / rho
-            mac[0, rows, :] = rho
-            mac[1, rows, :] = weight
-            for n in range(3):
-                mac[2 + n, rows, :] = momentum[n] * scale
-            for n, term in enumerate(momentum + [rho]):
-                term = term * weight
-                if n == 3:
-                    mac[5, rows, :] = term
-                high = term.astype(jnp.bfloat16).astype(jnp.float32)
-                split[pl.ds(8 * start + n, 8, stride=8), :] = high
-                split[pl.ds(8 * start + 4 + n, 8, stride=8), :] = term - high
-        return carry
-
-    lax.fori_loop(0, CX, moments, 0, unroll=2)
-
-    low_row = lax.broadcasted_iota(jnp.int32, (32, 128), 0)
-
-    def add_slab(x, total):
-        left, right = [], []
-        for y in range(CY):
-            slots = int_v[pl.ds(CY * x + y, 1), :]
-            tile = split[pl.ds(pl.multiple_of(8 * (CY * x + y), 8), 8), :]
-            upper = jnp.broadcast_to(slots >> 5, (8, 128))
-            picked = [jnp.where(upper == a, tile, 0.0) for a in range(8)]
-            left.append(jnp.concatenate(picked, axis=0).astype(jnp.bfloat16))
-            lower = jnp.broadcast_to(slots & 31, (32, 128))
-            right.append(jnp.where(lower == low_row, 1.0, 0.0).astype(jnp.bfloat16))
-        return total + dot_lanes(
-            jnp.concatenate(left, axis=1), jnp.concatenate(right, axis=1)
-        )
-
-    total = lax.fori_loop(0, CX, add_slab, jnp.zeros((64, 32), jnp.float32), unroll=4)
-    tables = []
-    for h in range(2):
-        table = jnp.concatenate(
-            [total[8 * a : 8 * a + 8, :] for a in range(4 * h, 4 * h + 4)], axis=1
-        )
-        tables.append(table + pltpu.roll(table, 4, 0))
-
-    for q in range(14):
-        source = inv_v[q]
-        index = source & 127
-        picked = jnp.where(
-            source < 128, lane_gather(tables[0], index), lane_gather(tables[1], index)
-        )
-        picked = jnp.where(source >= 0, picked, 0.0)
-        cs[2 * q] = picked[0:4, :]
-        cs[2 * q + 1] = picked[4:8, :]
 
     def send_c(code):
         return pltpu.make_async_remote_copy(
             src_ref=cs.at[code],
             dst_ref=cr.at[26 - code],
-            send_sem=c_send.at[code],
-            recv_sem=c_recv.at[26 - code],
+            send_sem=c_send,
+            recv_sem=c_recv,
             device_id=device(offset_of(code)),
             device_id_type=MESH,
         )
+
+    def partial_sums():
+        wait_rows(in_sem.at[1], 4 + CANDIDATES)
+        entry = touch_v[0:1, :]
+        wide = lax.broadcasted_iota(jnp.int32, (112, TOUCHES), 1)
+        row = lax.broadcasted_iota(jnp.int32, (112, TOUCHES), 0)
+        named = jnp.where((entry >> 7) == (row >> 2), wide + 1, 0).astype(jnp.float32)
+        slot_row = lax.broadcasted_iota(jnp.int32, (SLOTS, TOUCHES), 0)
+        placed = jnp.where((entry & 127) == slot_row, 1.0, 0.0)
+        inverse = dot_lanes(named.astype(jnp.bfloat16), placed.astype(jnp.bfloat16))
+        inv_v[...] = (inverse.astype(jnp.int32) - 1).reshape(14, 8, 128)
+        code_row = jnp.broadcast_to(dcode_v[0:1, :], (8, 128))
+        moved = jnp.concatenate(
+            [jnp.where(code_row == code, lane + 1, 0).astype(jnp.float32) for code in MOVE_CODES]
+            + [jnp.zeros((8, 128), jnp.float32)],
+            axis=0,
+        )
+        tall = lax.broadcasted_iota(jnp.int32, (SLOTS, SLOTS), 0)
+        landing = jnp.where(dslot_v[0:1, :] == tall, 1.0, 0.0)
+        inverse2 = dot_lanes(moved.astype(jnp.bfloat16), landing.astype(jnp.bfloat16))
+        inv2_v[...] = (inverse2.astype(jnp.int32) - 1).reshape(8, 8, 128)
+
+        wait_rows(in_sem.at[2], 2 * CX * CY)
+
+        def moments(x, carry):
+            for half in range(2):
+                start = pl.multiple_of(CY * x + 8 * half, 8)
+                rows = pl.ds(start, 8)
+                f = [f_v[d, rows, :] for d in range(19)]
+                rho = f[0]
+                momentum = [None, None, None]
+                for d in range(1, 19):
+                    rho = rho + f[d]
+                for n in range(3):
+                    for d in range(1, 19):
+                        if LATTICE[d][n] == 1:
+                            momentum[n] = f[d] if momentum[n] is None else momentum[n] + f[d]
+                    for d in range(1, 19):
+                        if LATTICE[d][n] == -1:
+                            momentum[n] = momentum[n] - f[d]
+                eps = frac_v[rows, :]
+                weight = jnp.where(
+                    int_v[rows, :] < TOUCHES,
+                    eps * (RELAX_TIME - 0.5) / (1.0 - eps + (RELAX_TIME - 0.5)),
+                    0.0,
+                )
+                scale = 1.0 / rho
+                mac[0, rows, :] = rho
+                mac[1, rows, :] = weight
+                for n in range(3):
+                    mac[2 + n, rows, :] = momentum[n] * scale
+                for n, term in enumerate(momentum + [rho]):
+                    term = term * weight
+                    if n == 3:
+                        mac[5, rows, :] = term
+                    high = term.astype(jnp.bfloat16).astype(jnp.float32)
+                    split[pl.ds(8 * start + n, 8, stride=8), :] = high
+                    split[pl.ds(8 * start + 4 + n, 8, stride=8), :] = term - high
+            return carry
+
+        for part_x in range(2):
+            pop_load(part_x).wait()
+            lax.fori_loop(4 * part_x, 4 * part_x + 4, moments, 0, unroll=2)
+
+        low_row = lax.broadcasted_iota(jnp.int32, (32, 128), 0)
+
+        def add_slab(x, total):
+            left, right = [], []
+            for y in range(CY):
+                slots = int_v[pl.ds(CY * x + y, 1), :]
+                tile = split[pl.ds(pl.multiple_of(8 * (CY * x + y), 8), 8), :]
+                upper = jnp.broadcast_to(slots >> 5, (8, 128))
+                picked = [jnp.where(upper == a, tile, 0.0) for a in range(8)]
+                left.append(jnp.concatenate(picked, axis=0).astype(jnp.bfloat16))
+                lower = jnp.broadcast_to(slots & 31, (32, 128))
+                right.append(jnp.where(lower == low_row, 1.0, 0.0).astype(jnp.bfloat16))
+            return total + dot_lanes(
+                jnp.concatenate(left, axis=1), jnp.concatenate(right, axis=1)
+            )
+
+        total = lax.fori_loop(0, CX, add_slab, jnp.zeros((64, 32), jnp.float32), unroll=4)
+        tables = []
+        for h in range(2):
+            table = jnp.concatenate(
+                [total[8 * a : 8 * a + 8, :] for a in range(4 * h, 4 * h + 4)], axis=1
+            )
+            tables.append(table + pltpu.roll(table, 4, 0))
+
+        for q in range(14):
+            source = inv_v[q]
+            index = source & 127
+            picked = jnp.where(
+                source < 128, lane_gather(tables[0], index), lane_gather(tables[1], index)
+            )
+            picked = jnp.where(source >= 0, picked, 0.0)
+            cs[2 * q] = picked[0:4, :]
+            cs[2 * q + 1] = picked[4:8, :]
+
+
+    early = (here[2] == 1) | (here[1] == 4) | ((here[0] < 3) & (lax.rem(here[1], 4) < 3))
+    pl.when(early)(partial_sums)
+
+    own_load.wait()
+    pl.semaphore_wait(barrier, neighbours)
+    start_all(send_a)
+    pl.when(jnp.logical_not(early))(partial_sums)
 
     start_all(send_c)
 
@@ -361,7 +370,7 @@
     lax.fori_loop(0, CX, pack_ends, 0, unroll=CX)
     zc[...] = jnp.transpose(zm[...])[0:16, :]
 
-    wait_all(send_a)
+    wait_all(a_recv, 8)
 
     for code in others:
         nb[code] = jnp.where(ok[code], nb[code], 0.0)
@@ -450,8 +459,8 @@
         return pltpu.make_async_remote_copy(
             src_ref=source,
             dst_ref=target,
-            send_sem=b_send.at[n],
-            recv_sem=b_recv.at[n],
+            send_sem=b_send,
+            recv_sem=b_recv,
             device_id=device(offset),
             device_id_type=MESH,
         )
@@ -462,22 +471,6 @@
     for n in range(len(moves)):
         pl.when(ok[code_of(moves[n][2])])(lambda n=n: send_b(n).start())
 
-    def solid(x, carry):
-        for half in range(2):
-            rows, dest = cell_rows(x, half)
-            v, base, even, odd = solid_part(int_v[rows, :], mac[5, rows, :])
-            rel[PLACE[0], dest, :] = rel[PLACE[0], dest, :] + WEIGHTS[0] * base
-            for i, j in PAIRS:
-                along = projected(v, i)
-                symmetric = WEIGHTS[i] * (base + even * along * along)
-                skew = WEIGHTS[i] * (odd * along)
-                rel[PLACE[i], dest, :] = rel[PLACE[i], dest, :] + (symmetric + skew)
-                rel[PLACE[j], dest, :] = rel[PLACE[j], dest, :] + (symmetric - skew)
-        return carry
-
-    lax.fori_loop(0, CX, solid, 0, unroll=CX)
-
-    loads[6].wait()
     listed = [
         cont_v[0:8, :],
         jnp.concatenate([cont_v[8:12, :], jnp.full((4, 128), 27 * SLOTS, jnp.int32)], axis=0),
@@ -512,7 +505,7 @@
             term = jnp.sum(apart[n] * strength, axis=0, keepdims=True)
             force[n] = term if h == 0 else force[n] + term
 
-    wait_all(send_c)
+    wait_all(c_recv, 4)
     hydro = cs[13]
     for code in others:
         hydro = hydro + jnp.where(ok[code], cr[code], 0.0)
@@ -539,8 +532,8 @@
         return pltpu.make_async_remote_copy(
             src_ref=ds.at[n],
             dst_ref=dr.at[6 - n],
-            send_sem=d_send.at[n],
-            recv_sem=d_recv.at[6 - n],
+            send_sem=d_send,
+            recv_sem=d_recv,
             device_id=device(offset_of(MOVE_CODES[n])),
             device_id_type=MESH,
         )
@@ -549,28 +542,35 @@
     for n in movers:
         pl.when(ok[MOVE_CODES[n]])(lambda n=n: send_d(n).start())
 
-    for n in movers:
-
-        @pl.when(ok[MOVE_CODES[n]])
-        def _(n=n):
-            send_d(6 - n).wait_recv()
-            send_d(n).wait_send()
-
+    def solid(x, carry):
+        for half in range(2):
+            rows, dest = cell_rows(x, half)
+            v, base, even, odd = solid_part(int_v[rows, :], mac[5, rows, :])
+            rel[PLACE[0], dest, :] = rel[PLACE[0], dest, :] + WEIGHTS[0] * base
+            for i, j in PAIRS:
+                along = projected(v, i)
+                symmetric = WEIGHTS[i] * (base + even * along * along)
+                skew = WEIGHTS[i] * (odd * along)
+                rel[PLACE[i], dest, :] = rel[PLACE[i], dest, :] + (symmetric + skew)
+                rel[PLACE[j], dest, :] = rel[PLACE[j], dest, :] + (symmetric - skew)
+        return carry
+
+    lax.fori_loop(0, CX, solid, 0, unroll=CX)
+
+    def side_rows(a, b, c):
+        return 8 * (10 * a + 5 * b + c + a * b + a * c + b * c)
+
+    wait_sides(b_recv, side_rows)
+    wait_sides(d_recv, lambda a, b, c: 8 * (a + b + c))
     arrived = ds[3]
     for n in movers:
         arrived = arrived + jnp.where(ok[MOVE_CODES[n]], dr[n], 0.0)
     out_part[0, 0, :, 0, :] = arrived[0:6, :]
 
-    for n in range(len(moves)):
-        there = moves[n][2]
-
-        @pl.when(ok[26 - code_of(there)])
-        def _(n=n):
-            send_b(n).wait_recv()
-
-        @pl.when(ok[code_of(there)])
-        def _(n=n):
-            send_b(n).wait_send()
+    wait_all(a_send, 8)
+    wait_all(c_send, 4)
+    wait_sides(b_send, side_rows)
+    wait_sides(d_send, lambda a, b, c: 8 * (a + b + c))
 
     for side in range(2):
         x = -1 if side == 0 else CX
@@ -601,7 +601,7 @@
 
 def stream_kernel(sizes, rel, columns, records, out_pop, out_part, out_v, out_sem, part_sem):
     here = [lax.axis_index(axis) for axis in AXES]
-    keep_records = pltpu.make_async_copy(records, out_part, part_sem.at[0])
+    keep_records = pltpu.make_async_copy(records, out_part, part_sem)
     keep_records.start()
     lane = lax.broadcasted_iota(jnp.int32, (8, 128), 1)
     sub = lax.broadcasted_iota(jnp.int32, (8, 128), 0)
@@ -610,7 +610,7 @@
     order = sorted(range(19), key=lambda d: LATTICE[d][2] != 0)
 
     def put(d):
-        return pltpu.make_async_copy(out_v.at[d], out_pop.at[d], out_sem.at[d])
+        return pltpu.make_async_copy(out_v.at[d], out_pop.at[d], out_sem)
 
     for d in order:
         vector = LATTICE[d]
@@ -645,8 +645,7 @@
                     value = jnp.where(blocked, back, value)
                 out_v[d, cells, :] = value
         put(d).start()
-    for d in order:
-        put(d).wait()
+    pltpu.make_async_copy(out_v, out_pop, out_sem).wait()
     keep_records.wait()
 
 
@@ -705,16 +704,15 @@
             vmem((8, 128), f32),
             vmem((7, 8, 128), f32),
             vmem((7, 8, 128), f32),
-            sems((7,)),
-            sems((CX,)),
-            sems((27,)),
-            sems((27,)),
-            sems((18,)),
-            sems((18,)),
-            sems((27,)),
-            sems((27,)),
-            sems((7,)),
-            sems((7,)),
+            sems((5,)),
+            sems,
+            sems,
+            sems,
+            sems,
+            sems,
+            sems,
+            sems,
+            sems,
         ],
         compiler_params=pltpu.CompilerParams(collective_id=0, has_side_effects=True),
     )(*args)
@@ -726,7 +724,7 @@
         ),
         in_specs=[in_vmem] * 3,
         out_specs=(in_any,) * 2,
-        scratch_shapes=[vmem((19, cells, CZ), f32), sems((19,)), sems((1,))],
+        scratch_shapes=[vmem((19, cells, CZ), f32), sems, sems],
     )(*(pltpu.with_memory_space_constraint(a, vmem) for a in (relaxed, columns, records)))
     return populations.reshape(19, CX, CY, CZ), jnp.transpose(records, (0, 1, 3, 2, 4))
 

time: 20.4 us -> 18.6 us (0.912)
  Pallas kernels: 19.6 us -> 17.8 us
    pallas_call x1, Pallas kernels: 18.4 us -> 16.7 us  [body(): pl.pallas_call(lambda *refs: kernel(sizes, *refs), out_shape=(vmem((19, S...]
where the time goes in v3:
time: 18.6 us; the launch traced here: 18.5 us
  Pallas kernels  17.8 us (96%)
  between operations  0.64 us (3%)
    pallas_call x1, Pallas kernels, body(): pl.pallas_call(lambda *refs: kernel(sizes, *refs), out_shape=(vmem((19, S...  16.7 us
    pallas_call x1, Pallas kernels, body(): pl.pallas_call(lambda *refs: stream_kernel(sizes, *refs), out_shape=(jax....  1.08 us

profile of v3, /device:TPU:1, one launch (start us, length us, event | category | flops | bytes accessed | tf_op | source)
XLA Modules:
  0.0 18.5 jit_solution(17147865357531089018)
XLA Ops:
  0.6 16.7 %shard_map.95 = (f32[19,320,128]{2,1,0:T(8,128)S(1)}, f32[128,128]{1,0:T(8,128)S(1)}, f32[1,1,6,1,128]{4,3,2,1,0:T(1,128)S(1)}) custom-call(f32[19,128,128]{2,1,0:T(8,128)} %bitcast.9, f32[128,128]{1,0:T(8,128)} %bitcast.10, s32[128,128]{1,0:T(8,128)} %bitcast.11, s32[1,1,1,256]{3,2,1,0:T(1,128)} %refs_3_.1, f32[1,1,6,1,128]{4,3,2,1,0:T(1,128)} %bitcast.13, ...), custom_call_target="tpu_custom_call" | custom-call | tf_op jit(solution)/shard_map/pallas_call | solution.py:670
  17.4 1.1 %shard_map.96 = (f32[19,128,128]{2,1,0:T(8,128)}, f32[1,1,6,1,128]{4,3,2,1,0:T(1,128)}) custom-call(f32[19,320,128]{2,1,0:T(8,128)S(1)} %get-tuple-element.7.refs_0_, f32[128,128]{1,0:T(8,128)S(1)} %get-tuple-element.8.refs_1_, f32[1,1,6,1,128]{4,3,2,1,0:T(1,128)S(1)} %get-tuple-element.9.refs_2_), custom_call_target="tpu_custom_call" | custom-call | tf_op jit(solution)/shard_map/pallas_call | solution.py:719

commit v4 on v3

--- a/solution.py
+++ b/solution.py
@@ -112,14 +112,11 @@
     ds,
     dr,
     in_sem,
-    a_send,
     a_recv,
-    b_send,
     b_recv,
-    c_send,
     c_recv,
-    d_send,
     d_recv,
+    sent,
 ):
     rel = rel_out
     here = [lax.axis_index(axis) for axis in AXES]
@@ -182,18 +179,12 @@
         (dcode.at[0, 0], dcode_v),
         (dslot.at[0, 0], dslot_v),
         (cont.at[0, 0, :, 0], cont_v),
+        (frac, frac_v),
+        (inter, int_v),
     ):
         pltpu.make_async_copy(source, target, in_sem.at[1]).start()
-    for source, target in ((frac, frac_v), (inter, int_v)):
-        pltpu.make_async_copy(source, target, in_sem.at[2]).start()
-
-    def pop_load(x):
-        return pltpu.make_async_copy(
-            pop.at[:, pl.ds(64 * x, 64)], f_v.at[:, pl.ds(64 * x, 64)], in_sem.at[3 + x]
-        )
-
-    for x in range(2):
-        pop_load(x).start()
+    pop_load = pltpu.make_async_copy(pop, f_v, in_sem.at[2])
+    pop_load.start()
 
     lane = lax.broadcasted_iota(jnp.int32, (8, 128), 1)
     sub = lax.broadcasted_iota(jnp.int32, (8, 128), 0)
@@ -202,8 +193,8 @@
         return pltpu.make_async_remote_copy(
             src_ref=nb.at[13],
             dst_ref=nb.at[26 - code],
-            send_sem=a_send,
-            recv_sem=a_recv,
+            send_sem=sent,
+            recv_sem=a_recv.at[int(0 not in offset_of(code))],
             device_id=device(offset_of(code)),
             device_id_type=MESH,
         )
@@ -212,14 +203,14 @@
         return pltpu.make_async_remote_copy(
             src_ref=cs.at[code],
             dst_ref=cr.at[26 - code],
-            send_sem=c_send,
+            send_sem=sent,
             recv_sem=c_recv,
             device_id=device(offset_of(code)),
             device_id_type=MESH,
         )
 
     def partial_sums():
-        wait_rows(in_sem.at[1], 4 + CANDIDATES)
+        wait_rows(in_sem.at[1], 4 + CANDIDATES + 2 * CX * CY)
         entry = touch_v[0:1, :]
         wide = lax.broadcasted_iota(jnp.int32, (112, TOUCHES), 1)
         row = lax.broadcasted_iota(jnp.int32, (112, TOUCHES), 0)
@@ -239,7 +230,7 @@
         inverse2 = dot_lanes(moved.astype(jnp.bfloat16), landing.astype(jnp.bfloat16))
         inv2_v[...] = (inverse2.astype(jnp.int32) - 1).reshape(8, 8, 128)
 
-        wait_rows(in_sem.at[2], 2 * CX * CY)
+        pop_load.wait()
 
         def moments(x, carry):
             for half in range(2):
@@ -277,9 +268,7 @@
                     split[pl.ds(8 * start + 4 + n, 8, stride=8), :] = term - high
             return carry
 
-        for part_x in range(2):
-            pop_load(part_x).wait()
-            lax.fori_loop(4 * part_x, 4 * part_x + 4, moments, 0, unroll=2)
+        lax.fori_loop(0, CX, moments, 0, unroll=2)
 
         low_row = lax.broadcasted_iota(jnp.int32, (32, 128), 0)
 
@@ -368,25 +357,48 @@
         return carry
 
     lax.fori_loop(0, CX, pack_ends, 0, unroll=CX)
-    zc[...] = jnp.transpose(zm[...])[0:16, :]
-
-    wait_all(a_recv, 8)
-
+    across = jnp.transpose(zm[...])
+
+    def at_target(tile):
+        up_y = jnp.where((lane & 15) == 0, pltpu.roll(tile, 128 - 15, 1), pltpu.roll(tile, 1, 1))
+        down_y = jnp.where((lane & 15) == 15, pltpu.roll(tile, 15, 1), pltpu.roll(tile, 127, 1))
+        moved_z = jnp.where(sub == 1, pltpu.roll(tile, 16, 1), tile)
+        moved_z = jnp.where(sub == 2, pltpu.roll(tile, 112, 1), moved_z)
+        moved_z = jnp.where(sub == 3, up_y, moved_z)
+        return jnp.where(sub == 4, down_y, moved_z)
+
+    for side in range(2):
+        zc[side, 0] = at_target(across[8 * side : 8 * side + 8, :])
+        for n in range(2):
+            line = across[8 * side + 5 + n : 8 * side + 6 + n, :]
+            zc[side, 1 + n] = at_target(jnp.broadcast_to(line, (8, 128)))
+
+    touch_code, touch_slot = (
+        [jnp.broadcast_to(part_of[:, 128 * h : 128 * h + 128], (8, 128)) for h in range(2)]
+        for part_of in (touch_v[0:1, :] >> 7, touch_v[0:1, :] & 127)
+    )
+    zero = jnp.zeros((8, 128), jnp.float32)
+    found = [zero, zero]
+
+    def find_velocity(code):
+        tile = nb[code]
+        if code != 13:
+            tile = jnp.where(ok[code], tile, 0.0)
+            nb[code] = tile
+        for h in range(2):
+            found[h] = jnp.where(
+                touch_code[h] == code, lane_gather(tile, touch_slot[h]), found[h]
+            )
+
+    corners = [code for code in others if 0 not in offset_of(code)]
+    wait_sides(a_recv.at[0], lambda a, b, c: 8 * ((a + 1) * (b + 1) * (c + 1) - 1 - a * b * c))
+    find_velocity(13)
     for code in others:
-        nb[code] = jnp.where(ok[code], nb[code], 0.0)
-
-    touch_code = [jnp.broadcast_to(touch_v[0:1, pl.ds(128 * h, 128)] >> 7, (8, 128)) for h in range(2)]
-    touch_slot = [jnp.broadcast_to(touch_v[0:1, pl.ds(128 * h, 128)] & 127, (8, 128)) for h in range(2)]
-
-    def find_velocity(code, found):
-        tile = nb[code]
-        return tuple(
-            jnp.where(touch_code[h] == code, lane_gather(tile, touch_slot[h]), found[h])
-            for h in range(2)
-        )
-
-    zero = jnp.zeros((8, 128), jnp.float32)
-    found = lax.fori_loop(0, 27, find_velocity, (zero, zero), unroll=27)
+        if code not in corners:
+            find_velocity(code)
+    wait_sides(a_recv.at[1], lambda a, b, c: 8 * a * b * c)
+    for code in corners:
+        find_velocity(code)
     speed = [
         [jnp.broadcast_to(SPEED_UNIT * found[h][3 + n : 4 + n, :], (8, 128)) for n in range(3)]
         for h in range(2)
@@ -407,6 +419,42 @@
         along = projected(v, d)
         return WEIGHTS[d] * (base + along * (even * along + odd))
 
+    def send_b(move):
+        source, target, offset = move
+        return pltpu.make_async_remote_copy(
+            src_ref=source,
+            dst_ref=target,
+            send_sem=sent,
+            recv_sem=b_recv.at[abs(offset[2])],
+            device_id=device(offset),
+            device_id_type=MESH,
+        )
+
+    def code_of(offset):
+        return 9 * (offset[0] + 1) + 3 * (offset[1] + 1) + offset[2] + 1
+
+    def start_b(moves):
+        for move in moves:
+            pl.when(ok[code_of(move[2])])(lambda move=move: send_b(move).start())
+
+    signs = [[jnp.zeros((8, 128), jnp.float32) for n in range(3)] for side in range(2)]
+    for side in range(2):
+        for n, d in enumerate(Z_MOVERS[side]):
+            for axis in range(3):
+                if LATTICE[d][axis] != 0:
+                    signs[side][axis] = jnp.where(
+                        sub == n, float(LATTICE[d][axis]), signs[side][axis]
+                    )
+    share = jnp.where(sub == 0, 1.0 / 18.0, 1.0 / 36.0)
+    for side in range(2):
+        v, base, even, odd = solid_part(zc[side, 2].astype(jnp.int32), zc[side, 1])
+        along = signs[side][0] * v[0] + signs[side][1] * v[1] + signs[side][2] * v[2]
+        zs[side] = zc[side, 0] + share * (base + along * (even * along + odd))
+    moves = []
+    for n, (step_x, step_y) in ((3, (0, -1)), (2, (0, 1)), (0, (1, 0)), (1, (-1, 0))):
+        for side in (1, 0):
+            moves.append((zs.at[side], ze.at[side, n], (step_x, step_y, 1 - 2 * side)))
+    start_b(moves)
     for side in range(2):
         x = CX - 1 if side == 0 else 0
         for half in range(2):
@@ -425,51 +473,16 @@
             if LATTICE[d][0] != 0:
                 value = pltpu.roll(value, LATTICE[d][0] % CX, 0)
             ys[side, n] = value
-    for side in range(2):
-        slots = jnp.broadcast_to(zc[8 * side + 6 : 8 * side + 7, :].astype(jnp.int32), (8, 128))
-        mass = jnp.broadcast_to(zc[8 * side + 5 : 8 * side + 6, :], (8, 128))
-        v, base, even, odd = solid_part(slots, mass)
-        along = zero
-        share = jnp.full((8, 128), 1.0 / 36.0, jnp.float32)
-        for n, d in enumerate(Z_MOVERS[side]):
-            along = jnp.where(sub == n, projected(v, d), along)
-        share = jnp.where(sub == 0, 1.0 / 18.0, share)
-        tile = zc[8 * side : 8 * side + 8, :] + share * (base + along * (even * along + odd))
-        up_y = jnp.where((lane & 15) == 0, pltpu.roll(tile, 128 - 15, 1), pltpu.roll(tile, 1, 1))
-        down_y = jnp.where((lane & 15) == 15, pltpu.roll(tile, 15, 1), pltpu.roll(tile, 127, 1))
-        moved_z = jnp.where(sub == 1, pltpu.roll(tile, 16, 1), tile)
-        moved_z = jnp.where(sub == 2, pltpu.roll(tile, 112, 1), moved_z)
-        moved_z = jnp.where(sub == 3, up_y, moved_z)
-        zs[side] = jnp.where(sub == 4, down_y, moved_z)
-
+    start_b([(xs.at[side], xr.at[side], (1 - 2 * side, 0, 0)) for side in (1, 0)])
     moves = []
-    for side in range(2):
+    for side in (1, 0):
         step = 1 - 2 * side
-        moves.append((xs.at[side], xr.at[side], (step, 0, 0)))
-        moves.append((ys.at[side], yr.at[side], (0, step, 0)))
         moves.append((ys.at[side, 1], ye.at[side, 0], (1, step, 0)))
         moves.append((ys.at[side, 2], ye.at[side, 1], (-1, step, 0)))
-        moves.append((zs.at[side], zr.at[side], (0, 0, step)))
-        moves.append((zs.at[side], ze.at[side, 0], (1, 0, step)))
-        moves.append((zs.at[side], ze.at[side, 1], (-1, 0, step)))
-        moves.append((zs.at[side], ze.at[side, 2], (0, 1, step)))
-        moves.append((zs.at[side], ze.at[side, 3], (0, -1, step)))
-    def send_b(n):
-        source, target, offset = moves[n]
-        return pltpu.make_async_remote_copy(
-            src_ref=source,
-            dst_ref=target,
-            send_sem=b_send,
-            recv_sem=b_recv,
-            device_id=device(offset),
-            device_id_type=MESH,
-        )
-
-    def code_of(offset):
-        return 9 * (offset[0] + 1) + 3 * (offset[1] + 1) + offset[2] + 1
-
-    for n in range(len(moves)):
-        pl.when(ok[code_of(moves[n][2])])(lambda n=n: send_b(n).start())
+    for side in (1, 0):
+        moves.append((ys.at[side], yr.at[side], (0, 1 - 2 * side, 0)))
+    start_b(moves)
+    start_b([(zs.at[side], zr.at[side], (0, 0, 1 - 2 * side)) for side in (1, 0)])
 
     listed = [
         cont_v[0:8, :],
@@ -532,7 +545,7 @@
         return pltpu.make_async_remote_copy(
             src_ref=ds.at[n],
             dst_ref=dr.at[6 - n],
-            send_sem=d_send,
+            send_sem=sent,
             recv_sem=d_recv,
             device_id=device(offset_of(MOVE_CODES[n])),
             device_id_type=MESH,
@@ -557,21 +570,13 @@
 
     lax.fori_loop(0, CX, solid, 0, unroll=CX)
 
-    def side_rows(a, b, c):
-        return 8 * (10 * a + 5 * b + c + a * b + a * c + b * c)
-
-    wait_sides(b_recv, side_rows)
-    wait_sides(d_recv, lambda a, b, c: 8 * (a + b + c))
-    arrived = ds[3]
-    for n in movers:
-        arrived = arrived + jnp.where(ok[MOVE_CODES[n]], dr[n], 0.0)
-    out_part[0, 0, :, 0, :] = arrived[0:6, :]
-
-    wait_all(a_send, 8)
-    wait_all(c_send, 4)
-    wait_sides(b_send, side_rows)
-    wait_sides(d_send, lambda a, b, c: 8 * (a + b + c))
-
+    def near_rows(a, b):
+        return 8 * (10 * a + 5 * b + a * b)
+
+    def far_rows(a, b, c):
+        return 8 * c * (1 + a + b)
+
+    wait_sides(b_recv.at[0], lambda a, b, c: near_rows(a, b))
     for side in range(2):
         x = -1 if side == 0 else CX
         for n, d in enumerate((X_UP, X_DOWN)[side]):
@@ -586,20 +591,30 @@
                 tile = jnp.where(sub == CX - 1, ye[side, 1], tile)
             start = STRIDE * (1 - LATTICE[d][0]) + PAD + y
             rel[PLACE[d], pl.ds(start, CX, stride=STRIDE), :] = tile
-    columns = []
+    wait_sides(d_recv, lambda a, b, c: 8 * (a + b + c))
+    arrived = ds[3]
+    for n in movers:
+        arrived = arrived + jnp.where(ok[MOVE_CODES[n]], dr[n], 0.0)
+    out_part[0, 0, :, 0, :] = arrived[0:6, :]
+
+    wait_sides(b_recv.at[1], far_rows)
     for side in range(2):
         tile = zr[side]
         tile = jnp.where((sub == 1) & (lane < CY), ze[side, 0], tile)
         tile = jnp.where((sub == 2) & (lane >= 128 - CY), ze[side, 1], tile)
         tile = jnp.where((sub == 3) & ((lane & 15) == 0), ze[side, 2], tile)
         tile = jnp.where((sub == 4) & ((lane & 15) == 15), ze[side, 3], tile)
-        columns.append(tile)
-    col_out[...] = jnp.transpose(
-        jnp.concatenate(columns + [jnp.zeros((112, 128), jnp.float32)], axis=0)
+        col_out[8 * side : 8 * side + 8, :] = tile
+    wait_sides(
+        sent,
+        lambda a, b, c: 12 * ((a + 1) * (b + 1) * (c + 1) - 1)
+        + near_rows(a, b)
+        + far_rows(a, b, c)
+        + 8 * (a + b + c),
     )
 
 
-def stream_kernel(sizes, rel, columns, records, out_pop, out_part, out_v, out_sem, part_sem):
+def stream_kernel(sizes, rel, ends, records, out_pop, out_part, out_v, out_sem, part_sem):
     here = [lax.axis_index(axis) for axis in AXES]
     keep_records = pltpu.make_async_copy(records, out_part, part_sem)
     keep_records.start()
@@ -614,6 +629,10 @@
 
     for d in order:
         vector = LATTICE[d]
+        if d == order[4]:
+            columns = jnp.transpose(
+                jnp.concatenate([ends[...], jnp.zeros((112, 128), jnp.float32)], axis=0)
+            )
         for x in range(CX):
             for half in range(2):
                 cells = pl.ds(CY * x + 8 * half, 8)
@@ -632,7 +651,7 @@
                     column = 8 * side + Z_MOVERS[side].index(d)
                     value = jnp.where(
                         lane == (0 if side == 0 else 127),
-                        columns[cells, column : column + 1],
+                        columns[CY * x + 8 * half : CY * x + 8 * half + 8, column : column + 1],
                         pltpu.roll(value, vector[2] % 128, 1),
                     )
                 blocked = None
@@ -671,7 +690,7 @@
         lambda *refs: kernel(sizes, *refs),
         out_shape=(
             vmem((19, STRIDE * (CX + 2), CZ), f32),
-            vmem((cells, 128), f32),
+            vmem((16, 128), f32),
             vmem((1, 1, 6, 1, SLOTS), f32),
         ),
         in_specs=[in_any] * 8,
@@ -691,7 +710,7 @@
             vmem((8, 8, 128), i32),
             vmem((28, 4, 128), f32),
             vmem((27, 4, 128), f32),
-            vmem((16, 128), f32),
+            vmem((2, 3, 8, 128), f32),
             vmem((2, 5, CY, CZ), f32),
             vmem((2, 5, CY, CZ), f32),
             vmem((2, 5, CX, CZ), f32),
@@ -704,12 +723,9 @@
             vmem((8, 128), f32),
             vmem((7, 8, 128), f32),
             vmem((7, 8, 128), f32),
-            sems((5,)),
-            sems,
-            sems,
-            sems,
-            sems,
-            sems,
+            sems((3,)),
+            sems((2,)),
+            sems((2,)),
             sems,
             sems,
             sems,

time: 18.6 us -> 18.1 us (0.973)
  Pallas kernels: 17.8 us -> 17.3 us
    pallas_call x1, Pallas kernels: 16.7 us -> 16.1 us  [body(): pl.pallas_call(lambda *refs: kernel(sizes, *refs), out_shape=(vmem((19, S...]
where the time goes in v4:
time: 18.1 us; the launch traced here: 17.9 us
  Pallas kernels  17.3 us (96%)
  between operations  0.64 us (4%)
    pallas_call x1, Pallas kernels, body(): pl.pallas_call(lambda *refs: kernel(sizes, *refs), out_shape=(vmem((19, S...  16.1 us
    pallas_call x1, Pallas kernels, body(): pl.pallas_call(lambda *refs: stream_kernel(sizes, *refs), out_shape=(jax....  1.13 us

profile of v4, /device:TPU:1, one launch (start us, length us, event | category | flops | bytes accessed | tf_op | source)
XLA Modules:
  0.0 17.9 jit_solution(10119358536632578647)
XLA Ops:
  0.6 16.1 %shard_map.95 = (f32[19,320,128]{2,1,0:T(8,128)S(1)}, f32[16,128]{1,0:T(8,128)S(1)}, f32[1,1,6,1,128]{4,3,2,1,0:T(1,128)S(1)}) custom-call(f32[19,128,128]{2,1,0:T(8,128)} %bitcast.9, f32[128,128]{1,0:T(8,128)} %bitcast.10, s32[128,128]{1,0:T(8,128)} %bitcast.11, s32[1,1,1,256]{3,2,1,0:T(1,128)} %refs_3_.1, f32[1,1,6,1,128]{4,3,2,1,0:T(1,128)} %bitcast.13, ...), custom_call_target="tpu_custom_call" | custom-call | tf_op jit(solution)/shard_map/pallas_call | solution.py:689
  16.8 1.1 %shard_map.96 = (f32[19,128,128]{2,1,0:T(8,128)}, f32[1,1,6,1,128]{4,3,2,1,0:T(1,128)}) custom-call(f32[19,320,128]{2,1,0:T(8,128)S(1)} %get-tuple-element.7.refs_0_, f32[16,128]{1,0:T(8,128)S(1)} %get-tuple-element.8.refs_1_, f32[1,1,6,1,128]{4,3,2,1,0:T(1,128)S(1)} %get-tuple-element.9.refs_2_), custom_call_target="tpu_custom_call" | custom-call | tf_op jit(solution)/shard_map/pallas_call | solution.py:735

commit v5 on v4

--- a/solution.py
+++ b/solution.py
@@ -183,8 +183,12 @@
         (inter, int_v),
     ):
         pltpu.make_async_copy(source, target, in_sem.at[1]).start()
-    pop_load = pltpu.make_async_copy(pop, f_v, in_sem.at[2])
-    pop_load.start()
+    def pop_load(n):
+        rows = pl.ds(64 * n, 64)
+        return pltpu.make_async_copy(pop.at[:, rows], f_v.at[:, rows], in_sem.at[2 + n])
+
+    for n in range(2):
+        pop_load(n).start()
 
     lane = lax.broadcasted_iota(jnp.int32, (8, 128), 1)
     sub = lax.broadcasted_iota(jnp.int32, (8, 128), 0)
@@ -230,7 +234,6 @@
         inverse2 = dot_lanes(moved.astype(jnp.bfloat16), landing.astype(jnp.bfloat16))
         inv2_v[...] = (inverse2.astype(jnp.int32) - 1).reshape(8, 8, 128)
 
-        pop_load.wait()
 
         def moments(x, carry):
             for half in range(2):
@@ -268,7 +271,9 @@
                     split[pl.ds(8 * start + 4 + n, 8, stride=8), :] = term - high
             return carry
 
-        lax.fori_loop(0, CX, moments, 0, unroll=2)
+        for n in range(2):
+            pop_load(n).wait()
+            lax.fori_loop(4 * n, 4 * n + 4, moments, 0, unroll=2)
 
         low_row = lax.broadcasted_iota(jnp.int32, (32, 128), 0)
 
@@ -286,7 +291,7 @@
                 jnp.concatenate(left, axis=1), jnp.concatenate(right, axis=1)
             )
 
-        total = lax.fori_loop(0, CX, add_slab, jnp.zeros((64, 32), jnp.float32), unroll=4)
+        total = lax.fori_loop(0, CX, add_slab, jnp.zeros((64, 32), jnp.float32), unroll=8)
         tables = []
         for h in range(2):
             table = jnp.concatenate(
@@ -305,7 +310,7 @@
             cs[2 * q + 1] = picked[4:8, :]
 
 
-    early = (here[2] == 1) | (here[1] == 4) | ((here[0] < 3) & (lax.rem(here[1], 4) < 3))
+    early = (here[2] == 1) | (here[1] == 4) | ((here[0] < 2) & (lax.rem(here[1], 4) < 2))
     pl.when(early)(partial_sums)
 
     own_load.wait()
@@ -473,7 +478,6 @@
             if LATTICE[d][0] != 0:
                 value = pltpu.roll(value, LATTICE[d][0] % CX, 0)
             ys[side, n] = value
-    start_b([(xs.at[side], xr.at[side], (1 - 2 * side, 0, 0)) for side in (1, 0)])
     moves = []
     for side in (1, 0):
         step = 1 - 2 * side
@@ -481,8 +485,11 @@
         moves.append((ys.at[side, 2], ye.at[side, 1], (-1, step, 0)))
     for side in (1, 0):
         moves.append((ys.at[side], yr.at[side], (0, 1 - 2 * side, 0)))
+    for side in (1, 0):
+        moves.append((xs.at[side], xr.at[side], (1 - 2 * side, 0, 0)))
+    for side in (1, 0):
+        moves.append((zs.at[side], zr.at[side], (0, 0, 1 - 2 * side)))
     start_b(moves)
-    start_b([(zs.at[side], zr.at[side], (0, 0, 1 - 2 * side)) for side in (1, 0)])
 
     listed = [
         cont_v[0:8, :],
@@ -723,7 +730,7 @@
             vmem((8, 128), f32),
             vmem((7, 8, 128), f32),
             vmem((7, 8, 128), f32),
-            sems((3,)),
+            sems((4,)),
             sems((2,)),
             sems((2,)),
             sems,

time: 18.1 us -> 18.1 us (level)
  no operation moved by 1% of the time
where the time goes in v5:
time: 18.1 us; the launch traced here: 17.9 us
  Pallas kernels  17.3 us (96%)
  between operations  0.64 us (4%)
    pallas_call x1, Pallas kernels, body(): pl.pallas_call(lambda *refs: kernel(sizes, *refs), out_shape=(vmem((19, S...  16.2 us
    pallas_call x1, Pallas kernels, body(): pl.pallas_call(lambda *refs: stream_kernel(sizes, *refs), out_shape=(jax....  1.13 us

profile of v5, /device:TPU:1, one launch (start us, length us, event | category | flops | bytes accessed | tf_op | source)
XLA Modules:
  0.0 17.9 jit_solution(15321462559993043246)
XLA Ops:
  0.6 16.2 %shard_map.95 = (f32[19,320,128]{2,1,0:T(8,128)S(1)}, f32[16,128]{1,0:T(8,128)S(1)}, f32[1,1,6,1,128]{4,3,2,1,0:T(1,128)S(1)}) custom-call(f32[19,128,128]{2,1,0:T(8,128)} %bitcast.9, f32[128,128]{1,0:T(8,128)} %bitcast.10, s32[128,128]{1,0:T(8,128)} %bitcast.11, s32[1,1,1,256]{3,2,1,0:T(1,128)} %refs_3_.1, f32[1,1,6,1,128]{4,3,2,1,0:T(1,128)} %bitcast.13, ...), custom_call_target="tpu_custom_call" | custom-call | tf_op jit(solution)/shard_map/pallas_call | solution.py:696
  16.8 1.1 %shard_map.96 = (f32[19,128,128]{2,1,0:T(8,128)}, f32[1,1,6,1,128]{4,3,2,1,0:T(1,128)}) custom-call(f32[19,320,128]{2,1,0:T(8,128)S(1)} %get-tuple-element.7.refs_0_, f32[16,128]{1,0:T(8,128)S(1)} %get-tuple-element.8.refs_1_, f32[1,1,6,1,128]{4,3,2,1,0:T(1,128)S(1)} %get-tuple-element.9.refs_2_), custom_call_target="tpu_custom_call" | custom-call | tf_op jit(solution)/shard_map/pallas_call | solution.py:742

commit v6 on v4

--- a/solution.py
+++ b/solution.py
@@ -305,7 +305,7 @@
             cs[2 * q + 1] = picked[4:8, :]
 
 
-    early = (here[2] == 1) | (here[1] == 4) | ((here[0] < 3) & (lax.rem(here[1], 4) < 3))
+    early = (here[2] == 1) | (here[1] == 4)
     pl.when(early)(partial_sums)
 
     own_load.wait()

time: 18.1 us -> 18 us (level)
  no operation moved by 1% of the time
where the time goes in v6:
time: 18 us; the launch traced here: 17.9 us
  Pallas kernels  17.3 us (96%)
  between operations  0.64 us (4%)
    pallas_call x1, Pallas kernels, body(): pl.pallas_call(lambda *refs: kernel(sizes, *refs), out_shape=(vmem((19, S...  16.1 us
    pallas_call x1, Pallas kernels, body(): pl.pallas_call(lambda *refs: stream_kernel(sizes, *refs), out_shape=(jax....  1.13 us

profile of v6, /device:TPU:1, one launch (start us, length us, event | category | flops | bytes accessed | tf_op | source)
XLA Modules:
  0.0 17.9 jit_solution(3095273162546393657)
XLA Ops:
  0.6 16.1 %shard_map.95 = (f32[19,320,128]{2,1,0:T(8,128)S(1)}, f32[16,128]{1,0:T(8,128)S(1)}, f32[1,1,6,1,128]{4,3,2,1,0:T(1,128)S(1)}) custom-call(f32[19,128,128]{2,1,0:T(8,128)} %bitcast.9, f32[128,128]{1,0:T(8,128)} %bitcast.10, s32[128,128]{1,0:T(8,128)} %bitcast.11, s32[1,1,1,256]{3,2,1,0:T(1,128)} %refs_3_.1, f32[1,1,6,1,128]{4,3,2,1,0:T(1,128)} %bitcast.13, ...), custom_call_target="tpu_custom_call" | custom-call | tf_op jit(solution)/shard_map/pallas_call | solution.py:689
  16.8 1.1 %shard_map.96 = (f32[19,128,128]{2,1,0:T(8,128)}, f32[1,1,6,1,128]{4,3,2,1,0:T(1,128)}) custom-call(f32[19,320,128]{2,1,0:T(8,128)S(1)} %get-tuple-element.7.refs_0_, f32[16,128]{1,0:T(8,128)S(1)} %get-tuple-element.8.refs_1_, f32[1,1,6,1,128]{4,3,2,1,0:T(1,128)S(1)} %get-tuple-element.9.refs_2_), custom_call_target="tpu_custom_call" | custom-call | tf_op jit(solution)/shard_map/pallas_call | solution.py:735
